TPU v7x, 8 devices: a whole 2x2x1 slice. The times are simulated.
8 devices in a mesh: dp: 2 (over z, y), ep: 4 (over x, core).
Axes of the slice: x: 2, y: 2, z: 1, core: 2. Of those that a mesh axis runs over, the one named last changes fastest.
Arguments:
- x_tokens: bfloat16 [1024, 2048], P(('dp', 'ep')), parts along dimension 0
- dy_tokens: bfloat16 [1024, 2048], P(('dp', 'ep')), parts along dimension 0
- expert_ids: int32 [1024, 10], P(('dp', 'ep')), parts along dimension 0
- gate_vals: float32 [1024, 10], P(('dp', 'ep')), parts along dimension 0
- slot_pos: int32 [1024, 10], P(('dp', 'ep')), parts along dimension 0
- w_gate: bfloat16 [32, 2048, 512], P('ep')
- w_up: bfloat16 [32, 2048, 512], P('ep')
- w_down: bfloat16 [32, 512, 2048], P('ep')
- shared_gate: bfloat16 [2048, 512], replicated
- shared_up: bfloat16 [2048, 512], replicated
- shared_down: bfloat16 [512, 2048], replicated
Outputs:
- output 1: bfloat16 [1024, 2048], P(('dp', 'ep')), parts along dimension 0
- output 2: float32 [64, 2048, 512], P(('dp', 'ep')), parts along dimension 0
- output 3: float32 [64, 2048, 512], P(('dp', 'ep')), parts along dimension 0
- output 4: float32 [64, 512, 2048], P(('dp', 'ep')), parts along dimension 0
- output 5: float32 [8, 2048, 512], P(('dp', 'ep')), parts along dimension 0
- output 6: float32 [8, 2048, 512], P(('dp', 'ep')), parts along dimension 0
- output 7: float32 [8, 512, 2048], P(('dp', 'ep')), parts along dimension 0
There are 2 independent parts. A program takes and returns all parts, laid end to end along the dimension named above; an argument that names none is the same for every part.
All inputs are finite; a program needn't handle non-finite values.
Results may differ from a plain program's by a relative error of at most 0.0104471.
Values are sent between devices in bfloat16 or wider.
A program may use at most 1 GiB of HBM per device.

v0:
```python
import jax
import jax.numpy as jnp
from jax import lax
from jax.sharding import PartitionSpec as P


def swiglu_parts(act_gate, act_up, grad_hidden):
    gate_f32 = act_gate.astype(jnp.float32)
    up_f32 = act_up.astype(jnp.float32)
    sigma = jax.nn.sigmoid(gate_f32)
    silu_gate = gate_f32 * sigma
    hidden = (silu_gate * up_f32).astype(jnp.bfloat16)
    grad_gate = (grad_hidden * up_f32 * sigma * (1.0 + gate_f32 * (1.0 - sigma))).astype(jnp.bfloat16)
    grad_up = (grad_hidden * silu_gate).astype(jnp.bfloat16)
    return hidden, grad_gate, grad_up


def slot_tables(expert_ids, slot_pos, gate_vals, num_experts, capacity):
    tok_count, top_k = expert_ids.shape
    slot_total = num_experts * capacity
    copy_slot = jnp.where(slot_pos >= 0, expert_ids * capacity + slot_pos, slot_total).reshape(-1)
    copy_token = jnp.broadcast_to(jnp.arange(tok_count, dtype=jnp.int32)[:, None], (tok_count, top_k)).reshape(-1)
    slot_token = jnp.full((slot_total + 1,), tok_count, jnp.int32).at[copy_slot].set(copy_token)[:slot_total]
    slot_gate = jnp.zeros((slot_total + 1,), jnp.float32).at[copy_slot].set(gate_vals.reshape(-1))[:slot_total]
    return copy_slot, slot_token, slot_gate


def take_rows(rows, row_index):
    return jnp.take(rows, row_index, axis=0, mode='fill', fill_value=0)


def shared_backward(x_tokens, dy_tokens, shared_gate, shared_up, shared_down):
    act_gate = jnp.dot(x_tokens, shared_gate, preferred_element_type=jnp.float32).astype(jnp.bfloat16)
    act_up = jnp.dot(x_tokens, shared_up, preferred_element_type=jnp.float32).astype(jnp.bfloat16)
    grad_hidden = jnp.einsum('td,fd->tf', dy_tokens, shared_down, preferred_element_type=jnp.float32)
    hidden, grad_gate, grad_up = swiglu_parts(act_gate, act_up, grad_hidden)
    grad_gate_w = jnp.einsum('td,tf->df', x_tokens, grad_gate, preferred_element_type=jnp.float32)
    grad_up_w = jnp.einsum('td,tf->df', x_tokens, grad_up, preferred_element_type=jnp.float32)
    grad_down_w = jnp.einsum('tf,td->fd', hidden, dy_tokens, preferred_element_type=jnp.float32)
    grad_input = jnp.einsum('tf,df->td', grad_gate, shared_gate, preferred_element_type=jnp.float32) + jnp.einsum('tf,df->td', grad_up, shared_up, preferred_element_type=jnp.float32)
    return grad_input, grad_gate_w, grad_up_w, grad_down_w


def solution(mesh):
    group = mesh.shape['ep']
    token_spec = P(('dp', 'ep'), None)
    expert_spec = P('ep', None, None)
    whole_spec = P(None, None)
    grad_spec = P(('dp', 'ep'), None, None)

    def local_backward(x_tokens, dy_tokens, expert_ids, gate_vals, slot_pos, w_gate, w_up, w_down, shared_gate, shared_up, shared_down):
        tok_count, top_k = expert_ids.shape
        local_experts, model_dim, expert_ff = w_gate.shape
        num_experts = local_experts * group
        capacity = (3 * tok_count * top_k + 2 * num_experts - 1) // (2 * num_experts)
        copy_slot, slot_token, slot_gate = slot_tables(expert_ids, slot_pos, gate_vals, num_experts, capacity)
        send_x = take_rows(x_tokens, slot_token).reshape(num_experts, capacity, model_dim)
        dy_rows = take_rows(dy_tokens, slot_token)
        send_dz = (dy_rows.astype(jnp.float32) * slot_gate[:, None]).astype(jnp.bfloat16).reshape(num_experts, capacity, model_dim)
        x_exp = lax.all_to_all(send_x, 'ep', 0, 1, tiled=True)
        dz_exp = lax.all_to_all(send_dz, 'ep', 0, 1, tiled=True)
        act_gate = jnp.einsum('erd,edf->erf', x_exp, w_gate, preferred_element_type=jnp.float32).astype(jnp.bfloat16)
        act_up = jnp.einsum('erd,edf->erf', x_exp, w_up, preferred_element_type=jnp.float32).astype(jnp.bfloat16)
        grad_hidden = jnp.einsum('erd,efd->erf', dz_exp, w_down, preferred_element_type=jnp.float32)
        hidden, grad_gate, grad_up = swiglu_parts(act_gate, act_up, grad_hidden)
        grad_w_gate = jnp.einsum('erd,erf->edf', x_exp, grad_gate, preferred_element_type=jnp.float32)
        grad_w_up = jnp.einsum('erd,erf->edf', x_exp, grad_up, preferred_element_type=jnp.float32)
        grad_w_down = jnp.einsum('erf,erd->efd', hidden, dz_exp, preferred_element_type=jnp.float32)
        grad_exp = (jnp.einsum('erf,edf->erd', grad_gate, w_gate, preferred_element_type=jnp.float32) + jnp.einsum('erf,edf->erd', grad_up, w_up, preferred_element_type=jnp.float32)).astype(jnp.bfloat16)
        returned = lax.all_to_all(grad_exp, 'ep', 1, 0, tiled=True).reshape(num_experts * capacity, model_dim)
        copies = take_rows(returned, copy_slot).reshape(tok_count, top_k, model_dim)
        routed_sum = jnp.sum(copies.astype(jnp.float32), axis=1)
        shared_dx, grad_shared_gate, grad_shared_up, grad_shared_down = shared_backward(x_tokens, dy_tokens, shared_gate, shared_up, shared_down)
        grad_x = (routed_sum + shared_dx).astype(jnp.bfloat16)
        return grad_x, grad_w_gate, grad_w_up, grad_w_down, grad_shared_gate[None], grad_shared_up[None], grad_shared_down[None]

    return jax.shard_map(local_backward, mesh=mesh, in_specs=(token_spec, token_spec, token_spec, token_spec, token_spec, expert_spec, expert_spec, expert_spec, whole_spec, whole_spec, whole_spec), out_specs=(token_spec, grad_spec, grad_spec, grad_spec, grad_spec, grad_spec, grad_spec), check_vma=False)
```

profile of v0, /device:TPU:0, one launch (start us, length us, event | category | flops | bytes accessed | tf_op | source)
XLA Modules:
  0.0 461.6 jit_solution(2861508257921472135)
XLA Ops:
  0.6 1.4 compare_and_fusion.1
  2.1 0.1 copy.40
  2.2 0.1 reshape.101
  2.3 0.6 fusion.34
  3.0 0.1 reshape.135
  3.1 5.2 %scatter_custom_fusion = s32[1921]{0:T(1024)S(1)} fusion(s32[1280]{0:T(1024)S(1)} %get-tuple-element.30, s32[1280]{0:T(1024)S(1)} %reshape.135, s32[]{:T(128)} %constant.14.clone.1), kind=kCustom, calls=%fused_computation.65 | custom fusion | bytes 7688 | tf_op jit(solution)/shard_map/scatter | solution.py:23
  8.4 17.4 %gather_fusion.2 = bf16[1920,2048]{1,0:T(8,128)(2,1)} fusion(bf16[128,2048]{1,0:T(8,128)(2,1)} %param.13, s32[2048]{0:T(1024)S(1)} %pad_clamp_fusion.1), kind=kCustom, calls=%fused_computation.1.clone | custom fusion | bytes 15736320 | tf_op jit(solution)/shard_map/jit(_take)/gather | solution.py:29
  25.8 7.1 %broadcast_select_fusion = bf16[1920,2048]{1,0:T(8,128)(2,1)} fusion(bf16[1920,2048]{1,0:T(8,128)(2,1)} %gather_fusion.2, pred[1920]{0:T(1024)(128)(4,1)S(1)} %compare_and_fusion), kind=kLoop, calls=%fused_computation.8 | loop fusion | flops 3932160 | bytes 15730560 | tf_op jit(solution)/shard_map/jit(_take)/select_n | solution.py:29
  32.8 9.1 %reshape.105 = bf16[32,60,2048]{2,1,0:T(8,128)(2,1)} reshape(bf16[1920,2048]{1,0:T(8,128)(2,1)} %broadcast_select_fusion) | data formatting | bytes 15728640 | tf_op jit(solution)/shard_map/reshape | solution.py:57
  42.0 5.7 %all-to-all-start.1 = ((bf16[32,60,2048]{2,1,0:T(8,128)(2,1)}), bf16[32,60,2048]{2,1,0:T(8,128)(2,1)}, u32[]{:S(2)}, u32[]{:S(2)}) async-start(bf16[32,60,2048]{2,1,0:T(8,128)(2,1)} %reshape.105), calls=%async_computation.1 | async-start | bytes 16777216 | tf_op jit(solution)/shard_map/all_to_all | solution.py:60
  47.7 8.6 %gather_fusion.1 = bf16[1920,2048]{1,0:T(8,128)(2,1)} fusion(bf16[128,2048]{1,0:T(8,128)(2,1)S(1)} %copy-done.3, s32[2048]{0:T(1024)S(1)} %pad_clamp_fusion.1), kind=kCustom, calls=%fused_computation.clone | custom fusion | bytes 15736320 | tf_op jit(solution)/shard_map/jit(_take)/gather | solution.py:29
  56.4 0.1 copy.41
  56.5 0.1 reshape.143
  56.6 5.2 %scatter_custom_fusion.1 = f32[1921]{0:T(1024)S(1)} fusion(s32[1280]{0:T(1024)S(1)} %get-tuple-element.30, f32[1280]{0:T(1024)S(1)} %reshape.143, f32[]{:T(128)} %constant.23.clone.1), kind=kCustom, calls=%fused_computation.63 | custom fusion | bytes 7688 | tf_op jit(solution)/shard_map/scatter | solution.py:24
  61.9 7.6 %multiply_convert_fusion = bf16[1920,2048]{1,0:T(8,128)(2,1)} fusion(bf16[1920,2048]{1,0:T(8,128)(2,1)} %gather_fusion.1, f32[1920]{0:T(1024)S(1)} %bitcast.50, pred[1920]{0:T(1024)(128)(4,1)S(1)} %compare_and_fusion), kind=kLoop, calls=%fused_computation.7 | loop fusion | flops 15728640 | bytes 15738240 | tf_op jit(solution)/shard_map/convert_element_type | solution.py:59
  69.5 9.1 %reshape.104 = bf16[32,60,2048]{2,1,0:T(8,128)(2,1)} reshape(bf16[1920,2048]{1,0:T(8,128)(2,1)} %multiply_convert_fusion) | data formatting | bytes 15728640 | tf_op jit(solution)/shard_map/reshape | solution.py:59
  78.6 63.0 %all-to-all-done.1 = bf16[32,60,2048]{2,1,0:T(8,128)(2,1)} async-done(((bf16[32,60,2048]{2,1,0:T(8,128)(2,1)}), bf16[32,60,2048]{2,1,0:T(8,128)(2,1)}, u32[]{:S(2)}, u32[]{:S(2)}) %all-to-all-start.1) | async-done | bytes 7864352 | tf_op jit(solution)/shard_map/all_to_all | solution.py:60
  141.6 5.9 %all-to-all-start = ((bf16[32,60,2048]{2,1,0:T(8,128)(2,1)}), bf16[32,60,2048]{2,1,0:T(8,128)(2,1)}, u32[]{:S(2)}, u32[]{:S(2)}) async-start(bf16[32,60,2048]{2,1,0:T(8,128)(2,1)} %reshape.104), calls=%async_computation | async-start | bytes 16777216 | tf_op jit(solution)/shard_map/all_to_all | solution.py:61
  147.5 0.4 fusion.29
  148.0 2.2 fusion.30
  150.2 0.9 multiply_convert_fusion.3
  151.1 2.7 convolution_bitcast_fusion.2
  153.8 2.8 convolution_bitcast_fusion.1
  156.6 2.8 convolution_bitcast_fusion
  159.4 1.8 fusion.42
  161.2 11.0 %copy.46 = bf16[8,4,60,2048]{3,0,2,1:T(8,128)(2,1)} copy(bf16[8,4,60,2048]{3,2,0,1:T(8,128)(2,1)} %bitcast.6) | data formatting | bytes 15728640 | tf_op jit(solution)/shard_map/all_to_all | solution.py:60
  172.2 17.7 %fusion.26 = bf16[8,240,512]{2,1,0:T(8,128)(2,1)S(1)} fusion(bf16[8,2048,512]{2,1,0:T(8,128)(2,1)} %param.18, bf16[8,240,2048]{2,0,1:T(8,128)(2,1)} %bitcast.44), kind=kOutput, calls=%fused_computation.42 | convolution fusion | flops 4027514880 | bytes 26607616 | tf_op jit(solution)/shard_map/erd,edf->erf/dot_general | solution.py:62
  189.8 18.7 %fusion.23 = bf16[8,240,512]{2,1,0:T(8,128)(2,1)} fusion(bf16[8,2048,512]{2,1,0:T(8,128)(2,1)} %param.19, bf16[8,240,2048]{2,0,1:T(8,128)(2,1)} %bitcast.45), kind=kOutput, calls=%fused_computation.41 | convolution fusion | flops 4027514880 | bytes 26607616 | tf_op jit(solution)/shard_map/erd,edf->erf/dot_general | solution.py:63
  208.6 31.5 %all-to-all-done = bf16[32,60,2048]{2,1,0:T(8,128)(2,1)} async-done(((bf16[32,60,2048]{2,1,0:T(8,128)(2,1)}), bf16[32,60,2048]{2,1,0:T(8,128)(2,1)}, u32[]{:S(2)}, u32[]{:S(2)}) %all-to-all-start) | async-done | bytes 7864352 | tf_op jit(solution)/shard_map/all_to_all | solution.py:61
  240.1 11.1 %copy.43 = bf16[8,4,60,2048]{3,0,2,1:T(8,128)(2,1)} copy(bf16[8,4,60,2048]{3,2,0,1:T(8,128)(2,1)} %bitcast.2) | data formatting | bytes 15728640 | tf_op jit(solution)/shard_map/all_to_all | solution.py:61
  251.2 21.9 %fusion.14 = (bf16[8,240,512]{2,1,0:T(8,128)(2,1)}, f32[8,240,512]{2,1,0:T(8,128)}) fusion(bf16[8,240,512]{2,1,0:T(8,128)(2,1)} %fusion.23, bf16[8,240,512]{2,1,0:T(8,128)(2,1)S(1)} %fusion.26, bf16[8,512,2048]{2,1,0:T(8,128)(2,1)} %param.20, bf16[8,240,2048]{2,0,1:T(8,128)(2,1)} %bitcast.48), kind=kOutput, calls=%fused_computation.28 | convolution fusion | flops 4038328320 | bytes 34471936 | tf_op jit(solution)/shard_map/erd,efd->erf/dot_general | solution.py:64
  273.1 12.2 %fusion.41 = f32[8,240,2048]{2,1,0:T(8,128)} fusion(bf16[8,240,512]{2,1,0:T(8,128)(2,1)} %get-tuple-element.35, bf16[8,2048,512]{2,1,0:T(8,128)(2,1)} %param.18), kind=kOutput, calls=%fused_computation.69 | convolution fusion | flops 4026531840 | bytes 34471936 | tf_op jit(solution)/shard_map/erf,edf->erd/dot_general | solution.py:69
  285.2 16.3 %add_convert_fusion = bf16[8,240,2048]{2,1,0:T(8,128)(2,1)} fusion(f32[8,240,2048]{2,1,0:T(8,128)} %fusion.41, bf16[8,2048,512]{2,1,0:T(8,128)(2,1)} %param.19, f32[8,240,512]{2,1,0:T(8,128)} %get-tuple-element.36, bf16[8,240,512]{2,1,0:T(8,128)(2,1)S(1)} %fusion.26), kind=kOutput, calls=%fused_computation.6 | convolution fusion | flops 4041277440 | bytes 46268416 | tf_op jit(solution)/shard_map/erf,edf->erd/dot_general | solution.py:69
  301.5 10.7 %copy.49 = bf16[8,240,2048]{2,0,1:T(8,128)(2,1)} copy(bf16[8,240,2048]{2,1,0:T(8,128)(2,1)} %add_convert_fusion) | data formatting | bytes 15728640 | tf_op jit(solution)/shard_map/convert_element_type | solution.py:69
  312.3 5.6 %all-to-all-start.2 = ((bf16[8,240,2048]{2,0,1:T(8,128)(2,1)}), bf16[8,240,2048]{2,0,1:T(8,128)(2,1)}, u32[]{:S(2)}, u32[]{:S(2)}) async-start(bf16[8,240,2048]{2,0,1:T(8,128)(2,1)} %copy.49), calls=%async_computation.2 | async-start | bytes 15728640 | tf_op jit(solution)/shard_map/all_to_all | solution.py:70
  318.0 0.1 copy.39
  318.1 5.3 %copy.54 = f32[1,2048,512]{2,1,0:T(8,128)} copy(f32[1,2048,512]{1,2,0:T(8,128)} %convolution_bitcast_fusion.2) | data formatting | bytes 8388608
  323.4 5.3 %copy.55 = f32[1,2048,512]{2,1,0:T(8,128)} copy(f32[1,2048,512]{1,2,0:T(8,128)} %convolution_bitcast_fusion.1) | data formatting | bytes 8388608
  328.8 23.4 %fusion.6 = f32[8,2048,512]{2,1,0:T(8,128)} fusion(bf16[8,240,512]{2,1,0:T(8,128)(2,1)} %get-tuple-element.35, bf16[8,240,2048]{2,0,1:T(8,128)(2,1)} %bitcast.46), kind=kOutput, calls=%fused_computation.18 | convolution fusion | flops 4026531840 | bytes 43384832 | tf_op jit(solution)/shard_map/erd,erf->edf/dot_general | solution.py:66
  352.2 26.8 %fusion = f32[8,512,2048]{2,1,0:T(8,128)} fusion(bf16[8,240,2048]{2,0,1:T(8,128)(2,1)} %bitcast.49, bf16[8,240,512]{2,1,0:T(8,128)(2,1)} %fusion.23, bf16[8,240,512]{2,1,0:T(8,128)(2,1)S(1)} %fusion.26), kind=kOutput, calls=%fused_computation.9 | convolution fusion | flops 4034396160 | bytes 45350912 | tf_op jit(solution)/shard_map/erf,erd->efd/dot_general | solution.py:68
  379.1 24.4 %fusion.4 = f32[8,2048,512]{2,1,0:T(8,128)} fusion(bf16[8,240,2048]{2,0,1:T(8,128)(2,1)} %bitcast.47, f32[8,240,512]{2,1,0:T(8,128)} %get-tuple-element.36, bf16[8,240,512]{2,1,0:T(8,128)(2,1)S(1)} %fusion.26), kind=kOutput, calls=%fused_computation.16 | convolution fusion | flops 4033413120 | bytes 47316992 | tf_op jit(solution)/shard_map/erd,erf->edf/dot_general | solution.py:67
  403.4 1.7 all-to-all-done.2
  405.1 11.1 %copy.50 = bf16[4,8,60,2048]{3,2,1,0:T(8,128)(2,1)} copy(bf16[4,8,60,2048]{3,1,2,0:T(8,128)(2,1)} %bitcast.9) | data formatting | bytes 15728640 | tf_op jit(solution)/shard_map/all_to_all | solution.py:70
  416.2 9.4 %reshape.106 = bf16[1920,2048]{1,0:T(8,128)(2,1)} reshape(bf16[4,8,60,2048]{3,2,1,0:T(8,128)(2,1)} %copy.50) | data formatting | bytes 15728640 | tf_op jit(solution)/shard_map/reshape | solution.py:70
  425.6 15.1 %gather_fusion = bf16[1280,2048]{1,0:T(8,128)(2,1)} fusion(bf16[1920,2048]{1,0:T(8,128)(2,1)} %reshape.106, s32[2048]{0:T(1024)S(1)} %pad_clamp_fusion), kind=kCustom, calls=%fused_computation.2 | custom fusion | bytes 10490880 | tf_op jit(solution)/shard_map/jit(_take)/gather | solution.py:29
  440.7 9.5 %gather.10 = bf16[128,10,2048]{2,1,0:T(8,128)(2,1)} reshape(bf16[1280,2048]{1,0:T(8,128)(2,1)} %gather_fusion) | data formatting | bytes 10485760 | tf_op jit(solution)/shard_map/jit(_take)/gather | solution.py:29
  450.3 9.3 %convert_reduce_fusion = f32[128,2048]{1,0:T(8,128)S(1)} fusion(bf16[128,10,2048]{2,1,0:T(8,128)(2,1)} %gather.10, pred[128,10]{1,0:T(8,128)(4,1)S(1)} %copy.39), kind=kLoop, calls=%fused_computation.5 | loop fusion | flops 7602176 | bytes 6292736 | tf_op jit(solution)/shard_map/reduce_sum | solution.py:72
  459.6 1.6 fusion.21
  (29 shorter events, 0.1 us)
Async XLA Ops:
  0.6 146.9 %copy-start = (bf16[2048,512]{1,0:T(8,128)(2,1)S(1)}, bf16[2048,512]{1,0:T(8,128)(2,1)}, u32[]{:S(2)}) copy-start(bf16[2048,512]{1,0:T(8,128)(2,1)} %param.21) | copy-start | bytes 6291460
  42.0 5.8 %copy-start.3 = (bf16[128,2048]{1,0:T(8,128)(2,1)S(1)}, bf16[128,2048]{1,0:T(8,128)(2,1)}, u32[]{:S(2)}) copy-start(bf16[128,2048]{1,0:T(8,128)(2,1)} %param.14) | copy-start | bytes 1572868
  42.0 99.6 %all-to-all-start.1 = ((bf16[32,60,2048]{2,1,0:T(8,128)(2,1)}), bf16[32,60,2048]{2,1,0:T(8,128)(2,1)}, u32[]{:S(2)}, u32[]{:S(2)}) async-start(bf16[32,60,2048]{2,1,0:T(8,128)(2,1)} %reshape.105), calls=%async_computation.1 | async-start | bytes 16777216 | tf_op jit(solution)/shard_map/all_to_all | solution.py:60
  47.7 8.7 %copy-start.9 = (f32[128,10]{0,1:T(8,128)S(1)}, f32[128,10]{0,1:T(8,128)}, u32[]{:S(2)}) copy-start(f32[128,10]{0,1:T(8,128)} %param.16) | copy-start | bytes 15364
  78.6 68.9 %copy-start.2 = (bf16[128,2048]{1,0:T(8,128)(2,1)S(1)}, bf16[128,2048]{1,0:T(8,128)(2,1)}, u32[]{:S(2)}) copy-start(bf16[128,2048]{1,0:T(8,128)(2,1)} %param.13) | copy-start | bytes 1572868
  141.6 98.5 %all-to-all-start = ((bf16[32,60,2048]{2,1,0:T(8,128)(2,1)}), bf16[32,60,2048]{2,1,0:T(8,128)(2,1)}, u32[]{:S(2)}, u32[]{:S(2)}) async-start(bf16[32,60,2048]{2,1,0:T(8,128)(2,1)} %reshape.104), calls=%async_computation | async-start | bytes 16777216 | tf_op jit(solution)/shard_map/all_to_all | solution.py:61
  147.5 2.7 copy-start.11
  151.1 5.5 %copy-start.6 = (bf16[128,512]{1,0:T(8,128)(2,1)}, bf16[128,512]{1,0:T(8,128)(2,1)S(1)}, u32[]{:S(2)}) copy-start(bf16[128,512]{1,0:T(8,128)(2,1)S(1)} %get-tuple-element.33) | copy-start | bytes 393220
  312.3 5.7 %copy-start.8 = (s32[1280]{0:T(1024)S(1)}, s32[1280]{0:T(1024)}, u32[]{:S(2)}) copy-start(s32[1280]{0:T(1024)} %get-tuple-element.29) | copy-start | bytes 15364
  312.3 5.7 %copy-start.10 = (pred[128,10]{0,1:T(8,128)(4,1)S(1)}, pred[128,10]{0,1:T(8,128)(4,1)}, u32[]{:S(2)}) copy-start(pred[128,10]{0,1:T(8,128)(4,1)} %get-tuple-element.31) | copy-start | bytes 3844
  312.3 92.9 %all-to-all-start.2 = ((bf16[8,240,2048]{2,0,1:T(8,128)(2,1)}), bf16[8,240,2048]{2,0,1:T(8,128)(2,1)}, u32[]{:S(2)}, u32[]{:S(2)}) async-start(bf16[8,240,2048]{2,0,1:T(8,128)(2,1)} %copy.49), calls=%async_computation.2 | async-start | bytes 15728640 | tf_op jit(solution)/shard_map/all_to_all | solution.py:70
  450.3 9.3 %copy-start.4 = (bf16[2048,512]{1,0:T(8,128)(2,1)S(1)}, bf16[2048,512]{1,0:T(8,128)(2,1)}, u32[]{:S(2)}) copy-start(bf16[2048,512]{1,0:T(8,128)(2,1)} %param.22) | copy-start | bytes 6291460
  450.3 9.3 %copy-start.5 = (f32[128,2048]{1,0:T(8,128)S(1)}, f32[128,2048]{1,0:T(8,128)}, u32[]{:S(2)}) copy-start(f32[128,2048]{1,0:T(8,128)} %fusion.42) | copy-start | bytes 3145732
  450.3 9.3 %copy-start.7 = (bf16[128,512]{1,0:T(8,128)(2,1)S(1)}, bf16[128,512]{1,0:T(8,128)(2,1)}, u32[]{:S(2)}) copy-start(bf16[128,512]{1,0:T(8,128)(2,1)} %copy-done.6) | copy-start | bytes 393220
  450.3 10.9 %copy-start.1 = (bf16[2048,512]{1,0:T(8,128)(2,1)S(1)}, bf16[2048,512]{1,0:T(8,128)(2,1)}, u32[]{:S(2)}) copy-start(bf16[2048,512]{1,0:T(8,128)(2,1)} %param.21) | copy-start | bytes 6291460
where the time goes:
time: 469 us; the launch traced here: 462 us
  matrix products  177 us (38%)
  local copies, waits for them, and re-layouts  144 us (31%)
  waiting for transfers between devices  96.2 us (21%)
  other arithmetic  26 us (6%)
  starting transfers between devices  17.3 us (4%)
    all_to_all x1, waiting for transfers between devices, local_backward(): x_exp = lax.all_to_all(send_x, 'ep', 0, 1, tiled=True)  63 us
    gather x4, local copies, waits for them, and re-layouts, take_rows(): return jnp.take(rows, row_index, axis=0, mode='fill', fill_value=0)  50.6 us
    all_to_all x1, waiting for transfers between devices, local_backward(): dz_exp = lax.all_to_all(send_dz, 'ep', 0, 1, tiled=True)  31.5 us
    dot_general x1, matrix products, local_backward(): jnp.einsum('erf,erd->efd', hidden, dz_exp, preferred_element_type=jnp.flo...  26.8 us
    dot_general x1, matrix products, local_backward(): jnp.einsum('erd,erf->edf', x_exp, grad_up, preferred_element_type=jnp.flo...  24.4 us
    dot_general x1, matrix products, local_backward(): jnp.einsum('erd,erf->edf', x_exp, grad_gate, preferred_element_type=jnp.f...  23.4 us
    dot_general x1, matrix products, local_backward(): jnp.einsum('erd,efd->erf', dz_exp, w_down, preferred_element_type=jnp.flo...  21.9 us
    dot_general x1, matrix products, local_backward(): jnp.einsum('erd,edf->erf', x_exp, w_up, preferred_element_type=jnp.float32)  18.7 us
  transfers between devices with their start and end apart: 3, of which 3 were waited for; matrix products, arithmetic and copies ran while one was open for 38% of the time, Pallas kernels for 0%

commit v1 on v0

v1 whole, which is shorter than its diff:
```python
import jax
import jax.numpy as jnp
from jax import lax
from jax.experimental import pallas as pl
from jax.experimental.pallas import tpu as pltpu
from jax.sharding import PartitionSpec as P


F32, BF16 = jnp.float32, jnp.bfloat16
SLOTS = 64


def dot(a, b):
    return jnp.dot(a, b, preferred_element_type=F32)


def dot_nt(a, b):
    return lax.dot_general(a, b, (((1,), (1,)), ((), ())), preferred_element_type=F32)


def dot_tt(a, b):
    return lax.dot_general(a, b, (((0,), (1,)), ((), ())), preferred_element_type=F32)


def swiglu_parts(a, b, g):
    a, b = a.astype(F32), b.astype(F32)
    sigma = jax.nn.sigmoid(a)
    silu = a * sigma
    hidden = (silu * b).astype(BF16)
    grad_a = (g * b * sigma * (1.0 + a * (1.0 - sigma))).astype(BF16)
    grad_b = (g * silu).astype(BF16)
    return hidden, grad_a, grad_b


def shared_kernel(x, dy, w1, w3, w2, rt, dw1, dw3, dw2):
    at = dot(x[...], w1[...]).astype(BF16).astype(F32).T
    bt = dot(x[...], w3[...]).astype(BF16).astype(F32).T
    gt = dot_nt(w2[...], dy[...])
    ht, dat, dbt = swiglu_parts(at, bt, gt)
    dw1[0] = dot_tt(x[...], dat)
    dw3[0] = dot_tt(x[...], dbt)
    dw2[0] = dot(ht, dy[...])
    part = dot(w1[...], dat) + dot(w3[...], dbt)

    @pl.when(pl.program_id(0) == 0)
    def _():
        rt[...] = part

    @pl.when(pl.program_id(0) != 0)
    def _():
        rt[...] += part


def shared_call(x, dy, w1, w3, w2):
    toks, d = x.shape
    ff = w1.shape[1]
    fb = ff // 2
    return pl.pallas_call(
        shared_kernel,
        grid=(ff // fb,),
        in_specs=[pl.BlockSpec((toks, d), lambda i: (0, 0)), pl.BlockSpec((toks, d), lambda i: (0, 0)), pl.BlockSpec((d, fb), lambda i: (0, i)), pl.BlockSpec((d, fb), lambda i: (0, i)), pl.BlockSpec((fb, d), lambda i: (i, 0))],
        out_specs=[pl.BlockSpec((d, toks), lambda i: (0, 0)), pl.BlockSpec((1, d, fb), lambda i: (0, 0, i)), pl.BlockSpec((1, d, fb), lambda i: (0, 0, i)), pl.BlockSpec((1, fb, d), lambda i: (0, i, 0))],
        out_shape=[jax.ShapeDtypeStruct((d, toks), F32), jax.ShapeDtypeStruct((1, d, ff), F32), jax.ShapeDtypeStruct((1, d, ff), F32), jax.ShapeDtypeStruct((1, ff, d), F32)],
        compiler_params=pltpu.CompilerParams(vmem_limit_bytes=56 * 2**20),
        cost_estimate=pl.CostEstimate(flops=16 * toks * d * ff, bytes_accessed=20 * 2**20, transcendentals=0),
        name='shared',
    )(x, dy, w1, w3, w2)


def one_hot_rows(slot_row, toks):
    rows = lax.broadcasted_iota(jnp.int32, (SLOTS, toks), 0).astype(F32)
    return rows == slot_row


def dispatch(tabs, toks, first, pick, rows_out, gated):
    experts = rows_out.shape[0]
    n, d = toks[0].shape
    cols = 512
    for q in range(len(toks)):
        gates = []
        for e in range(experts):
            hit = one_hot_rows(tabs[q][0, pl.ds(first + e, 1), :], n)
            pick[q, e * SLOTS:(e + 1) * SLOTS, :] = jnp.where(hit, 1.0, 0.0).astype(BF16)
            if gated:
                gates.append(jnp.sum(jnp.where(hit, tabs[q][1, pl.ds(first + e, 1), :], 0.0), axis=1, keepdims=True))

        def chunk(c, carry):
            at = pl.ds(pl.multiple_of(c * cols, cols), cols)
            got = dot(pick[q], toks[q][:, at])
            for e in range(experts):
                part = got[e * SLOTS:(e + 1) * SLOTS]
                if gated:
                    part = part * gates[e]
                rows_out[e, q * SLOTS:(q + 1) * SLOTS, at] = part.astype(BF16)
            return carry

        lax.fori_loop(0, d // cols, chunk, 0)


def forward_kernel(first, t0, t1, t2, t3, x0, x1, x2, x3, w1, w3, at, bt, x_out, rows, pick, sem):
    e = pl.program_id(0)
    copy = pltpu.make_async_copy(rows, x_out, sem)

    @pl.when(e == 0)
    def _():
        dispatch((t0, t1, t2, t3), (x0, x1, x2, x3), first[0], pick, rows, False)
        copy.start()

    at[0] = dot(rows[e], w1[0]).T.astype(BF16)
    bt[0] = dot(rows[e], w3[0]).T.astype(BF16)

    @pl.when(e == pl.num_programs(0) - 1)
    def _():
        copy.wait()


def whole(shape):
    return pl.BlockSpec(shape, lambda e: (0,) * len(shape))


def block(shape):
    return pl.BlockSpec((1,) + shape, lambda e: (e,) + (0,) * len(shape))


def forward_call(first, tabs, toks, w1, w3):
    experts, d, ff = w1.shape
    n = toks[0].shape[0]
    rows = SLOTS * len(toks)
    return pl.pallas_call(
        forward_kernel,
        grid=(experts,),
        in_specs=[pl.BlockSpec(memory_space=pltpu.SMEM)] + [whole(t.shape) for t in tabs] + [whole(t.shape) for t in toks] + [block((d, ff)), block((d, ff))],
        out_specs=[block((ff, rows)), block((ff, rows)), pl.BlockSpec(memory_space=pl.ANY)],
        out_shape=[jax.ShapeDtypeStruct((experts, ff, rows), BF16)] * 2 + [jax.ShapeDtypeStruct((experts, rows, d), BF16)],
        scratch_shapes=[pltpu.VMEM((experts, rows, d), BF16), pltpu.VMEM((len(toks), experts * SLOTS, n), BF16), pltpu.SemaphoreType.DMA],
        compiler_params=pltpu.CompilerParams(vmem_limit_bytes=56 * 2**20),
        cost_estimate=pl.CostEstimate(flops=4 * experts * rows * d * ff, bytes_accessed=48 * 2**20, transcendentals=0),
        name='forward',
    )(first, *tabs, *toks, w1, w3)


def backward_kernel(first, t0, t1, t2, t3, y0, y1, y2, y3, at, bt, w1, w3, w2, dat_out, dbt_out, dw2, keep, send, rows, pick, ret, spread):
    e = pl.program_id(0)
    experts = pl.num_programs(0)

    @pl.when(e == 0)
    def _():
        dispatch((t0, t1, t2, t3), (y0, y1, y2, y3), first[0], pick, rows, True)

    z = rows[e]
    gt = dot_nt(w2[0], z)
    ht, dat, dbt = swiglu_parts(at[0], bt[0], gt)
    dat_out[0] = dat
    dbt_out[0] = dbt
    dw2[0] = dot(ht, z)
    back = (dot(w1[0], dat) + dot(w3[0], dbt)).astype(BF16)
    lanes = pl.ds(pl.multiple_of(e * 2 * SLOTS, 2 * SLOTS), 2 * SLOTS)
    for p in range(2):
        ret[p, :, lanes] = back[:, p * 2 * SLOTS:(p + 1) * 2 * SLOTS]

    @pl.when(e == experts - 1)
    def _():
        n = y0.shape[0]
        d = y0.shape[1]
        count = rows.shape[0]
        for p in range(2):
            spread[p] = jnp.zeros_like(spread[p])
            for k in range(count):
                for h in range(2):
                    spread[p, k * 2 * SLOTS + h * SLOTS:k * 2 * SLOTS + (h + 1) * SLOTS, h * n:(h + 1) * n] = pick[2 * p + h, k * SLOTS:(k + 1) * SLOTS, :]

            def chunk(c, carry):
                m = pl.ds(pl.multiple_of(c * 512, 512), 512)
                tot = dot(ret[p, m, :], spread[p])
                keep[p, m, :] = tot[:, :n]
                send[p, m, :] = tot[:, n:]
                return carry

            lax.fori_loop(0, d // 512, chunk, 0)


def backward_call(first, tabs, toks, at, bt, w1, w3, w2):
    experts, d, ff = w1.shape
    n = toks[0].shape[0]
    rows = SLOTS * len(toks)
    return pl.pallas_call(
        backward_kernel,
        grid=(experts,),
        in_specs=[pl.BlockSpec(memory_space=pltpu.SMEM)] + [whole(t.shape) for t in tabs] + [whole(t.shape) for t in toks] + [block((ff, rows)), block((ff, rows)), block((d, ff)), block((d, ff)), block((ff, d))],
        out_specs=[block((ff, rows)), block((ff, rows)), block((ff, d)), whole((2, d, n)), whole((2, d, n))],
        out_shape=[jax.ShapeDtypeStruct((experts, ff, rows), BF16)] * 2 + [jax.ShapeDtypeStruct((experts, ff, d), F32)] + [jax.ShapeDtypeStruct((2, d, n), F32)] * 2,
        scratch_shapes=[pltpu.VMEM((experts, rows, d), BF16), pltpu.VMEM((len(toks), experts * SLOTS, n), BF16), pltpu.VMEM((2, d, experts * 2 * SLOTS), BF16), pltpu.VMEM((2, experts * 2 * SLOTS, 2 * n), BF16)],
        compiler_params=pltpu.CompilerParams(vmem_limit_bytes=60 * 2**20),
        cost_estimate=pl.CostEstimate(flops=8 * experts * rows * d * ff, bytes_accessed=96 * 2**20, transcendentals=0),
        name='backward',
    )(first, *tabs, *toks, at, bt, w1, w3, w2)


def weight_kernel(x, dat, dbt, dw1, dw3):
    dw1[0] = dot_tt(x[0], dat[0])
    dw3[0] = dot_tt(x[0], dbt[0])


def weight_call(x, dat, dbt):
    experts, rows, d = x.shape
    ff = dat.shape[1]
    return pl.pallas_call(
        weight_kernel,
        grid=(experts,),
        in_specs=[block((rows, d)), block((ff, rows)), block((ff, rows))],
        out_specs=[block((d, ff)), block((d, ff))],
        out_shape=[jax.ShapeDtypeStruct((experts, d, ff), F32)] * 2,
        compiler_params=pltpu.CompilerParams(vmem_limit_bytes=56 * 2**20),
        cost_estimate=pl.CostEstimate(flops=4 * experts * rows * d * ff, bytes_accessed=80 * 2**20, transcendentals=0),
        name='weights',
    )(x, dat, dbt)


def final_kernel(own, back, shared, out):
    out[...] = (own[0] + back[...] + shared[...]).T.astype(BF16)


def final_call(own, back, shared):
    d, n = shared.shape
    db = 512
    return pl.pallas_call(
        final_kernel,
        grid=(d // db,),
        in_specs=[pl.BlockSpec((1, db, n), lambda i: (0, i, 0)), pl.BlockSpec((db, n), lambda i: (i, 0)), pl.BlockSpec((db, n), lambda i: (i, 0))],
        out_specs=pl.BlockSpec((n, db), lambda i: (0, i)),
        out_shape=jax.ShapeDtypeStruct((n, d), BF16),
        name='final',
    )(own, back, shared)


def solution(mesh):
    token_spec = P(('dp', 'ep'), None)
    expert_spec = P('ep', None, None)
    whole_spec = P(None, None)
    grad_spec = P(('dp', 'ep'), None, None)
    group = mesh.shape['ep']

    def swap(v, bit):
        return lax.ppermute(v, 'ep', [(i, i ^ bit) for i in range(group)])

    def local_backward(x, dy, expert_ids, gate_vals, slot_pos, w1, w3, w2, s1, s3, s2):
        local = w1.shape[0]
        num_experts = local * group
        ids_t, slots_t, gates_t = expert_ids.T, slot_pos.T, gate_vals.T
        chosen = ids_t[:, None, :] == jnp.arange(num_experts, dtype=jnp.int32)[None, :, None]
        slot_tab = jnp.max(jnp.where(chosen, slots_t[:, None, :], -1), axis=0).astype(F32)
        gate_tab = jnp.sum(jnp.where(chosen, gates_t[:, None, :], 0.0), axis=0)
        tab = jnp.stack([slot_tab, gate_tab])
        first = (lax.axis_index('ep') * local).astype(jnp.int32).reshape(1)

        x, dy, tab = lax.optimization_barrier((x, dy, tab))
        t1, t2, t3 = swap(tab, 1), swap(tab, 2), swap(tab, 3)
        x2 = swap(x, 2)
        x1 = swap(x, 1)
        dy2 = swap(dy, 2)
        dy1 = swap(dy, 1)
        x3 = swap(x2, 1)
        dy3 = swap(dy2, 1)
        shared_t, ds1, ds3, ds2 = shared_call(x, dy, s1, s3, s2)
        tabs = (tab, t1, t2, t3)
        at, bt, x_rows = forward_call(first, tabs, (x, x1, x2, x3), w1, w3)
        dat, dbt, dw2, keep, send = backward_call(first, tabs, (dy, dy1, dy2, dy3), at, bt, w1, w3, w2)
        chip = keep + swap(send, 1)
        back = swap(chip[1], 2)
        dw1, dw3 = weight_call(x_rows, dat, dbt)
        grad_x = final_call(chip, back, shared_t)
        return grad_x, dw1, dw3, dw2, ds1, ds3, ds2

    return jax.shard_map(local_backward, mesh=mesh, in_specs=(token_spec, token_spec, token_spec, token_spec, token_spec, expert_spec, expert_spec, expert_spec, whole_spec, whole_spec, whole_spec), out_specs=(token_spec, grad_spec, grad_spec, grad_spec, grad_spec, grad_spec, grad_spec), check_vma=False)
```

time: 469 us -> 156 us (0.33); the launches traced: 462 us -> 155 us
  matrix products: 177 us -> 0 us
  local copies, waits for them, and re-layouts: 144 us -> 2.98 us
  Pallas kernels: 0 us -> 114 us
  waiting for transfers between devices: 96.2 us -> 25 us
  other arithmetic: 26 us -> 3.35 us
  starting transfers between devices: 17.3 us -> 9.46 us
    dot_general x16 -> x0, matrix products: 177 us -> none  [the longest x1 26.8 us: local_backward(): jnp.einsum('erf,erd->efd', hidden, dz_exp, preferred_element_type=jnp.flo...]
    pallas_call x0 -> x5, Pallas kernels: none -> 114 us  [the longest x1 48.7 us: backward_call(): pl.pallas_call(backward_kernel, grid=(experts,), in_specs=[pl.BlockSpec(m...]
    all_to_all x3 -> x0, waiting for transfers between devices: 96.2 us -> none  [the longest x1 63 us: local_backward(): x_exp = lax.all_to_all(send_x, 'ep', 0, 1, tiled=True)]
    gather x4 -> x0, local copies, waits for them, and re-layouts: 50.6 us -> none  [take_rows(): return jnp.take(rows, row_index, axis=0, mode='fill', fill_value=0)]
    all_to_all x3 -> x0, local copies, waits for them, and re-layouts: 33.2 us -> none  [the longest x1 11.1 us: local_backward(): dz_exp = lax.all_to_all(send_dz, 'ep', 0, 1, tiled=True)]
    reshape x6 -> x0, local copies, waits for them, and re-layouts: 28.1 us -> none  [the longest x1 9.4 us: local_backward(): lax.all_to_all(grad_exp, 'ep', 1, 0, tiled=True)]
    ppermute x0 -> x11, waiting for transfers between devices: none -> 25 us  [swap(): return lax.ppermute(v, 'ep', [(i, i ^ bit) for i in range(group)])]
    all_to_all x3 -> x0, starting transfers between devices: 17.3 us -> none  [the longest x1 5.86 us: local_backward(): dz_exp = lax.all_to_all(send_dz, 'ep', 0, 1, tiled=True)]
  transfers between devices with their start and end apart: 3 -> 11, of which waited for: 3 -> 3; matrix products, arithmetic and copies ran while one was open for 38% -> 0% of each run, Pallas kernels for 0% -> 40%
where the time goes in v1:
time: 156 us; the launch traced here: 155 us
  Pallas kernels  114 us (73%)
  waiting for transfers between devices  25 us (16%)
  starting transfers between devices  9.46 us (6%)
  other arithmetic  3.35 us (2%)
  local copies, waits for them, and re-layouts  2.98 us (2%)
    pallas_call x1, Pallas kernels, backward_call(): pl.pallas_call(backward_kernel, grid=(experts,), in_specs=[pl.BlockSpec(m...  48.7 us
    pallas_call x1, Pallas kernels, weight_call(): pl.pallas_call(weight_kernel, grid=(experts,), in_specs=[block((rows, d))...  25.9 us
    ppermute x11, waiting for transfers between devices, swap(): return lax.ppermute(v, 'ep', [(i, i ^ bit) for i in range(group)])  25 us
    pallas_call x1, Pallas kernels, forward_call(): pl.pallas_call(forward_kernel, grid=(experts,), in_specs=[pl.BlockSpec(me...  24.4 us
    pallas_call x1, Pallas kernels, shared_call(): pl.pallas_call(shared_kernel, grid=(ff // fb,), in_specs=[pl.BlockSpec((t...  11.2 us
    ppermute x11, starting transfers between devices, swap(): return lax.ppermute(v, 'ep', [(i, i ^ bit) for i in range(group)])  9.46 us
    pallas_call x1, Pallas kernels, final_call(): pl.pallas_call(final_kernel, grid=(d // db,), in_specs=[pl.BlockSpec((1,...  3.8 us
  transfers between devices with their start and end apart: 11, of which 3 were waited for; matrix products, arithmetic and copies ran while one was open for 0% of the time, Pallas kernels for 40%

profile of v1, /device:TPU:0, one launch (start us, length us, event | category | flops | bytes accessed | tf_op | source)
XLA Modules:
  0.0 155.5 jit_solution(14957923047312450708)
XLA Ops:
  0.6 0.7 select_reduce_fusion.1
  1.4 0.7 select_reduce_fusion
  2.2 3.3 %collective-permute-start.7 = (bf16[128,2048]{1,0:T(8,128)(2,1)}, bf16[128,2048]{1,0:T(8,128)(2,1)S(1)}, u32[]{:S(2)}, u32[]{:S(2)}) collective-permute-start(bf16[128,2048]{1,0:T(8,128)(2,1)} %x), channel_id=1, source_target_pairs={{0,2},{1,3},{2,0},{3,1},{4,6},{5,7},{6,4},{7,5}} | collective-permute-start | bytes 1572872 | tf_op jit(solution)/shard_map/ppermute | solution.py:244
  5.5 0.0 collective-permute-start.4
  5.5 0.0 collective-permute-start.6
  5.5 12.9 %collective-permute-done.7.x2 = bf16[128,2048]{1,0:T(8,128)(2,1)S(1)} collective-permute-done((bf16[128,2048]{1,0:T(8,128)(2,1)}, bf16[128,2048]{1,0:T(8,128)(2,1)S(1)}, u32[]{:S(2)}, u32[]{:S(2)}) %collective-permute-start.7) | collective-permute-done | bytes 524320 | tf_op jit(solution)/shard_map/ppermute | solution.py:244
  18.5 0.0 collective-permute-start.8
  18.5 0.5 collective-permute-start
  19.0 2.0 %collective-permute-start.1 = (f32[2,32,128]{2,1,0:T(8,128)S(1)}, f32[2,32,128]{2,1,0:T(8,128)S(1)}, u32[]{:S(2)}, u32[]{:S(2)}) collective-permute-start(f32[2,32,128]{2,1,0:T(8,128)S(1)} %pad_maximum_fusion.t0), channel_id=1, source_target_pairs={{0,2},{1,3},{2,0},{3,1},{4,6},{5,7},{6,4},{7,5}} | collective-permute-start | bytes 98312 | tf_op jit(solution)/shard_map/ppermute | solution.py:244
  21.0 0.0 collective-permute-done.t1
  21.0 1.2 collective-permute-start.2
  22.2 7.7 %collective-permute-done.1.t2 = f32[2,32,128]{2,1,0:T(8,128)S(1)} collective-permute-done((f32[2,32,128]{2,1,0:T(8,128)S(1)}, f32[2,32,128]{2,1,0:T(8,128)S(1)}, u32[]{:S(2)}, u32[]{:S(2)}) %collective-permute-start.1) | collective-permute-done | bytes 32800 | tf_op jit(solution)/shard_map/ppermute | solution.py:244
  29.9 0.0 collective-permute-start.3
  29.9 0.0 collective-permute-done.4.y2
  29.9 0.0 copy-start.9
  29.9 0.5 collective-permute-start.5
  30.4 0.0 collective-permute-done.2.t3
  30.4 0.0 collective-permute-done.6.x1
  30.4 0.0 copy-start.3
  30.5 0.0 collective-permute-done.8.x3
  30.5 0.0 copy-start.4
  30.5 0.0 copy-done.5
  30.5 0.0 copy-done.2
  30.5 0.0 copy-done.6
  30.5 0.0 copy-done.7
  30.5 0.5 copy-done.8
  31.0 0.2 copy-done.3
  31.2 0.2 copy-done.4
  31.4 24.4 %forward.1 = (bf16[8,512,256]{2,1,0:T(8,128)(2,1)}, bf16[8,512,256]{2,1,0:T(8,128)(2,1)}, bf16[8,256,2048]{2,1,0:T(8,128)(2,1)}) custom-call(s32[1]{0:T(128)} %bitcast.first, f32[2,32,128]{2,1,0:T(8,128)} %copy-done.5, f32[2,32,128]{2,1,0:T(8,128)} %copy-done.6, f32[2,32,128]{2,1,0:T(8,128)} %copy-done.7, f32[2,32,128]{2,1,0:T(8,128)} %copy-done.8, ...), custom_call_target="tpu_custom_call" | custom-call | flops 8589934592 | bytes 50331648 | tf_op jit(solution)/shard_map/forward/pallas_call | solution.py:129
  55.8 0.0 copy-done.9
  55.8 0.0 collective-permute-done.3.y1
  55.8 0.0 copy-start.10
  55.8 0.0 collective-permute-done.5.y3
  55.8 0.0 copy-start.11
  55.8 0.8 copy-done.10
  56.6 0.2 copy-done.11
  56.8 48.7 %backward.1 = (bf16[8,512,256]{2,1,0:T(8,128)(2,1)}, bf16[8,512,256]{2,1,0:T(8,128)(2,1)}, f32[8,512,2048]{2,1,0:T(8,128)}, f32[2,2048,128]{2,1,0:T(8,128)}, f32[2,2048,128]{2,1,0:T(8,128)}) custom-call(s32[1]{0:T(128)} %bitcast.first, f32[2,32,128]{2,1,0:T(8,128)} %copy-done.5, f32[2,32,128]{2,1,0:T(8,128)} %copy-done.6, f32[2,32,128]{2,1,0:T(8,128)} %copy-done.7, ...), custom_call_target="tpu_custom_call" | custom-call | flops 17179869184 | bytes 100663296 | tf_op jit(solution)/shard_map/backward/pallas_call | solution.py:186
  105.5 0.1 collective-permute-start.9
  105.6 4.3 %collective-permute-done.9 = f32[2,2048,128]{2,1,0:T(8,128)S(1)} collective-permute-done((f32[2,2048,128]{2,1,0:T(8,128)}, f32[2,2048,128]{2,1,0:T(8,128)S(1)}, u32[]{:S(2)}, u32[]{:S(2)}) %collective-permute-start.9) | collective-permute-done | bytes 2097184 | tf_op jit(solution)/shard_map/ppermute | solution.py:244
  109.9 1.9 %add.3.own = f32[2,2048,128]{2,1,0:T(8,128)S(1)} add(f32[2,2048,128]{2,1,0:T(8,128)} %get-tuple-element.29, f32[2,2048,128]{2,1,0:T(8,128)S(1)} %collective-permute-done.9) | non-fusion elementwise | flops 524288 | bytes 6291456 | tf_op jit(solution)/shard_map/add | solution.py:268
  111.8 0.1 slice_bitcast_fusion
  111.8 1.8 %collective-permute-start.10 = (f32[2048,128]{1,0:T(8,128)S(1)}, f32[2048,128]{1,0:T(8,128)S(1)}, u32[]{:S(2)}, u32[]{:S(2)}) collective-permute-start(f32[2048,128]{1,0:T(8,128)S(1)} %slice_bitcast_fusion), channel_id=1, source_target_pairs={{0,2},{1,3},{2,0},{3,1},{4,6},{5,7},{6,4},{7,5}} | collective-permute-start | bytes 3145736 | tf_op jit(solution)/shard_map/ppermute | solution.py:244
  113.6 11.2 %shared.1 = (f32[2048,128]{1,0:T(8,128)}, f32[1,2048,512]{2,1,0:T(8,128)}, f32[1,2048,512]{2,1,0:T(8,128)}, f32[1,512,2048]{2,1,0:T(8,128)}) custom-call(bf16[128,2048]{1,0:T(8,128)(2,1)} %x, bf16[128,2048]{1,0:T(8,128)(2,1)} %dy, bf16[2048,512]{1,0:T(8,128)(2,1)} %w1.5, bf16[2048,512]{1,0:T(8,128)(2,1)} %w3.5, bf16[512,2048]{1,0:T(8,128)(2,1)} %w2.3), custom_call_target="tpu_custom_call" | custom-call | flops 2147483648 | bytes 20971520 | tf_op jit(solution)/shard_map/shared/pallas_call | solution.py:58
  124.8 0.0 copy-done
  124.8 25.9 %weights.1 = (f32[8,2048,512]{2,1,0:T(8,128)}, f32[8,2048,512]{2,1,0:T(8,128)}) custom-call(bf16[8,256,2048]{2,1,0:T(8,128)(2,1)} %get-tuple-element.32.x, bf16[8,512,256]{2,1,0:T(8,128)(2,1)} %get-tuple-element.33.dat, bf16[8,512,256]{2,1,0:T(8,128)(2,1)} %get-tuple-element.34.dbt), custom_call_target="tpu_custom_call" | custom-call | flops 8589934592 | bytes 83886080 | tf_op jit(solution)/shard_map/weights/pallas_call | solution.py:207
  150.7 0.0 collective-permute-done.10.back
  150.7 1.0 copy-done.1
  151.7 3.8 %final.1 = bf16[128,2048]{1,0:T(8,128)(2,1)} custom-call(f32[2,2048,128]{2,1,0:T(8,128)} %copy-done, f32[2048,128]{1,0:T(8,128)} %copy-done.1, f32[2048,128]{1,0:T(8,128)} %get-tuple-element.31.shared), custom_call_target="tpu_custom_call" | custom-call | tf_op jit(solution)/shard_map/final/pallas_call | solution.py:226
  (9 shorter events, 0.0 us)
Async XLA Ops:
  2.1 28.3 %copy-start.5 = (f32[2,32,128]{2,1,0:T(8,128)}, f32[2,32,128]{2,1,0:T(8,128)S(1)}, u32[]{:S(2)}) copy-start(f32[2,32,128]{2,1,0:T(8,128)S(1)} %pad_maximum_fusion.t0) | copy-start | bytes 98308
  2.2 16.3 %collective-permute-start.7 = (bf16[128,2048]{1,0:T(8,128)(2,1)}, bf16[128,2048]{1,0:T(8,128)(2,1)S(1)}, u32[]{:S(2)}, u32[]{:S(2)}) collective-permute-start(bf16[128,2048]{1,0:T(8,128)(2,1)} %x), channel_id=1, source_target_pairs={{0,2},{1,3},{2,0},{3,1},{4,6},{5,7},{6,4},{7,5}} | collective-permute-start | bytes 1572872 | tf_op jit(solution)/shard_map/ppermute | solution.py:244
  5.5 24.4 %collective-permute-start.4 = (bf16[128,2048]{1,0:T(8,128)(2,1)}, bf16[128,2048]{1,0:T(8,128)(2,1)S(1)}, u32[]{:S(2)}, u32[]{:S(2)}) collective-permute-start(bf16[128,2048]{1,0:T(8,128)(2,1)} %dy), channel_id=1, source_target_pairs={{0,2},{1,3},{2,0},{3,1},{4,6},{5,7},{6,4},{7,5}} | collective-permute-start | bytes 1572872 | tf_op jit(solution)/shard_map/ppermute | solution.py:244
  5.5 24.9 %collective-permute-start.6 = (bf16[128,2048]{1,0:T(8,128)(2,1)}, bf16[128,2048]{1,0:T(8,128)(2,1)S(1)}, u32[]{:S(2)}, u32[]{:S(2)}) collective-permute-start(bf16[128,2048]{1,0:T(8,128)(2,1)} %x), channel_id=1, source_target_pairs={{0,1},{1,0},{2,3},{3,2},{4,5},{5,4},{6,7},{7,6}} | collective-permute-start | bytes 1572872 | tf_op jit(solution)/shard_map/ppermute | solution.py:244
  18.5 12.0 %copy-start.2 = (bf16[128,2048]{1,0:T(8,128)(2,1)}, bf16[128,2048]{1,0:T(8,128)(2,1)S(1)}, u32[]{:S(2)}) copy-start(bf16[128,2048]{1,0:T(8,128)(2,1)S(1)} %collective-permute-done.7.x2) | copy-start | bytes 1572868
  18.5 12.0 %collective-permute-start.8 = (bf16[128,2048]{1,0:T(8,128)(2,1)S(1)}, bf16[128,2048]{1,0:T(8,128)(2,1)S(1)}, u32[]{:S(2)}, u32[]{:S(2)}) collective-permute-start(bf16[128,2048]{1,0:T(8,128)(2,1)S(1)} %collective-permute-done.7.x2), channel_id=1, source_target_pairs={{0,1},{1,0},{2,3},{3,2},{4,5},{5,4},{6,7},{7,6}} | collective-permute-start | bytes 1572872 | tf_op jit(solution)/shard_map/ppermute | solution.py:244
  18.5 2.5 %collective-permute-start = (f32[2,32,128]{2,1,0:T(8,128)S(1)}, f32[2,32,128]{2,1,0:T(8,128)S(1)}, u32[]{:S(2)}, u32[]{:S(2)}) collective-permute-start(f32[2,32,128]{2,1,0:T(8,128)S(1)} %pad_maximum_fusion.t0), channel_id=1, source_target_pairs={{0,1},{1,0},{2,3},{3,2},{4,5},{5,4},{6,7},{7,6}} | collective-permute-start | bytes 98312 | tf_op jit(solution)/shard_map/ppermute | solution.py:244
  19.0 10.9 %collective-permute-start.1 = (f32[2,32,128]{2,1,0:T(8,128)S(1)}, f32[2,32,128]{2,1,0:T(8,128)S(1)}, u32[]{:S(2)}, u32[]{:S(2)}) collective-permute-start(f32[2,32,128]{2,1,0:T(8,128)S(1)} %pad_maximum_fusion.t0), channel_id=1, source_target_pairs={{0,2},{1,3},{2,0},{3,1},{4,6},{5,7},{6,4},{7,5}} | collective-permute-start | bytes 98312 | tf_op jit(solution)/shard_map/ppermute | solution.py:244
  21.0 9.5 %copy-start.6 = (f32[2,32,128]{2,1,0:T(8,128)}, f32[2,32,128]{2,1,0:T(8,128)S(1)}, u32[]{:S(2)}) copy-start(f32[2,32,128]{2,1,0:T(8,128)S(1)} %collective-permute-done.t1) | copy-start | bytes 98308
  21.0 9.4 %collective-permute-start.2 = (f32[2,32,128]{2,1,0:T(8,128)S(1)}, f32[2,32,128]{2,1,0:T(8,128)S(1)}, u32[]{:S(2)}, u32[]{:S(2)}) collective-permute-start(f32[2,32,128]{2,1,0:T(8,128)S(1)} %pad_maximum_fusion.t0), channel_id=1, source_target_pairs={{0,3},{1,2},{2,1},{3,0},{4,7},{5,6},{6,5},{7,4}} | collective-permute-start | bytes 98312 | tf_op jit(solution)/shard_map/ppermute | solution.py:244
  29.9 0.6 copy-start.7
  29.9 25.9 %collective-permute-start.3 = (bf16[128,2048]{1,0:T(8,128)(2,1)}, bf16[128,2048]{1,0:T(8,128)(2,1)S(1)}, u32[]{:S(2)}, u32[]{:S(2)}) collective-permute-start(bf16[128,2048]{1,0:T(8,128)(2,1)} %dy), channel_id=1, source_target_pairs={{0,1},{1,0},{2,3},{3,2},{4,5},{5,4},{6,7},{7,6}} | collective-permute-start | bytes 1572872 | tf_op jit(solution)/shard_map/ppermute | solution.py:244
  29.9 25.9 %copy-start.9 = (bf16[128,2048]{1,0:T(8,128)(2,1)}, bf16[128,2048]{1,0:T(8,128)(2,1)S(1)}, u32[]{:S(2)}) copy-start(bf16[128,2048]{1,0:T(8,128)(2,1)S(1)} %collective-permute-done.4.y2) | copy-start | bytes 1572868
  29.9 25.9 %collective-permute-start.5 = (bf16[128,2048]{1,0:T(8,128)(2,1)S(1)}, bf16[128,2048]{1,0:T(8,128)(2,1)S(1)}, u32[]{:S(2)}, u32[]{:S(2)}) collective-permute-start(bf16[128,2048]{1,0:T(8,128)(2,1)S(1)} %collective-permute-done.4.y2), channel_id=1, source_target_pairs={{0,1},{1,0},{2,3},{3,2},{4,5},{5,4},{6,7},{7,6}} | collective-permute-start | bytes 1572872 | tf_op jit(solution)/shard_map/ppermute | solution.py:244
  30.4 0.6 copy-start.8
  30.4 0.8 copy-start.3
  30.5 0.9 copy-start.4
  55.8 0.8 copy-start.10
  55.8 1.0 copy-start.11
  105.5 4.4 %collective-permute-start.9 = (f32[2,2048,128]{2,1,0:T(8,128)}, f32[2,2048,128]{2,1,0:T(8,128)S(1)}, u32[]{:S(2)}, u32[]{:S(2)}) collective-permute-start(f32[2,2048,128]{2,1,0:T(8,128)} %get-tuple-element.30), channel_id=1, source_target_pairs={{0,1},{1,0},{2,3},{3,2},{4,5},{5,4},{6,7},{7,6}} | collective-permute-start | bytes 6291464 | tf_op jit(solution)/shard_map/ppermute | solution.py:244
  111.8 13.0 %copy-start = (f32[2,2048,128]{2,1,0:T(8,128)}, f32[2,2048,128]{2,1,0:T(8,128)S(1)}, u32[]{:S(2)}) copy-start(f32[2,2048,128]{2,1,0:T(8,128)S(1)} %add.3.own) | copy-start | bytes 6291460
  111.8 38.9 %collective-permute-start.10 = (f32[2048,128]{1,0:T(8,128)S(1)}, f32[2048,128]{1,0:T(8,128)S(1)}, u32[]{:S(2)}, u32[]{:S(2)}) collective-permute-start(f32[2048,128]{1,0:T(8,128)S(1)} %slice_bitcast_fusion), channel_id=1, source_target_pairs={{0,2},{1,3},{2,0},{3,1},{4,6},{5,7},{6,4},{7,5}} | collective-permute-start | bytes 3145736 | tf_op jit(solution)/shard_map/ppermute | solution.py:244
  150.7 1.0 copy-start.1

commit v2 on v0

v2 whole, which is shorter than its diff:
```python
import jax
import jax.numpy as jnp
from jax import lax
from jax.experimental import pallas as pl
from jax.experimental.pallas import tpu as pltpu
from jax.sharding import PartitionSpec as P


F32, BF16 = jnp.float32, jnp.bfloat16
MESH = pl.DeviceIdType.MESH
SLOTS = 64
COLS = 512
RING, RING2 = 12, 8


def dot(a, b):
    return jnp.dot(a, b, preferred_element_type=F32)


def dot_nt(a, b):
    return lax.dot_general(a, b, (((1,), (1,)), ((), ())), preferred_element_type=F32)


def dot_tt(a, b):
    return lax.dot_general(a, b, (((0,), (1,)), ((), ())), preferred_element_type=F32)


def span(index, size):
    return pl.ds(pl.multiple_of(index * size, size), size)


def swiglu_parts(a, b, g):
    a, b = a.astype(F32), b.astype(F32)
    sigma = jax.nn.sigmoid(a)
    silu = a * sigma
    hidden = (silu * b).astype(BF16)
    grad_a = (g * b * sigma * (1.0 + a * (1.0 - sigma))).astype(BF16)
    grad_b = (g * silu).astype(BF16)
    return hidden, grad_a, grad_b


def make_picks(tabs, first, pick, gate):
    experts = pick.shape[1] // SLOTS
    toks = pick.shape[2]
    rows = lax.broadcasted_iota(jnp.int32, (SLOTS, toks), 0).astype(F32)
    for q in range(pick.shape[0]):
        def one(e, carry):
            hit = rows == tabs[q][0, pl.ds(first + e, 1), :]
            pick[q, span(e, SLOTS), :] = jnp.where(hit, 1.0, 0.0).astype(BF16)
            gate[q, span(e, SLOTS), :] = jnp.sum(jnp.where(hit, tabs[q][1, pl.ds(first + e, 1), :], 0.0), axis=1, keepdims=True)
            return carry

        lax.fori_loop(0, experts, one, 0)


def put_rows(got, q, rows):
    for e in range(rows.shape[0]):
        rows[e, q * SLOTS:(q + 1) * SLOTS, :] = got[e * SLOTS:(e + 1) * SLOTS]


def exchange_kernel(x, dy, tab, w1, w3, w2, s1, s3, s2, dat_o, dbt_o, ht_o, xg_o, yg_o, tg_o, sdat_o, sdbt_o, sht_o, own, far,
                    xg, yg, tg, wring, w2ring, s1v, s3v, s2v, acc, gacc, act, rows, pick, gate, ret, spread, sbuf, rbuf,
                    near_s, near_r, far_s, far_r, hop_s, hop_r, tab_s, tab_r, sum_s, sum_r, wsem, w2sem, ssem, osem):
    me = lax.axis_index('ep')
    core = me % 2
    mate = me + 1 - 2 * core
    other = (me + 2) % 4
    diag = (mate + 2) % 4
    experts, d, _ = w1.shape
    n = x.shape[0]
    chunks = d // COLS
    pieces = chunks * experts
    first = me * experts

    barrier = pltpu.get_barrier_semaphore()
    for peer in (mate, other, diag):
        pl.semaphore_signal(barrier, inc=1, device_id={'ep': peer}, device_id_type=MESH)
    pl.semaphore_wait(barrier, 3)

    def remote(src, dst, send, recv, peer):
        return pltpu.make_async_remote_copy(src_ref=src, dst_ref=dst, send_sem=send, recv_sem=recv, device_id={'ep': peer}, device_id_type=MESH)

    own_of, got_of = (x, dy), (xg, yg)

    def far_copy(a, c):
        return remote(own_of[a].at[:, span(c, COLS)], got_of[a].at[0, :, span(c, COLS)], far_s.at[a, c], far_r.at[a, c], other)

    def near_copy(a):
        return remote(own_of[a], got_of[a].at[1], near_s.at[a], near_r.at[a], mate)

    def hop_copy(a, c):
        return remote(got_of[a].at[0, :, span(c, COLS)], got_of[a].at[2, :, span(c, COLS)], hop_s.at[a, c], hop_r.at[a, c], mate)

    def tab_copy(k):
        return remote(tab, tg.at[k], tab_s.at[k], tab_r.at[k], (other, mate, diag)[k])

    def sum_copy(m):
        return remote(sbuf.at[m], rbuf.at[m], sum_s.at[m], sum_r.at[m], mate)

    def w_copy(i, k):
        src = (w1, w3)[k].at[i % experts, span((i // experts) % chunks, COLS), :]
        return pltpu.make_async_copy(src, wring.at[i % RING, k], wsem.at[i % RING, k])

    def w2_copy(j):
        return pltpu.make_async_copy(w2.at[j % experts, :, span(j // experts, COLS)], w2ring.at[j % RING2], w2sem.at[j % RING2])

    def s_copy(k):
        return pltpu.make_async_copy((s1, s3, s2)[k], (s1v, s3v, s2v)[k], ssem.at[k])

    def each(count, body):
        def step(i, carry):
            body(i)
            return carry

        lax.fori_loop(0, count, step, 0)

    for k in range(3):
        tab_copy(k).start()
    each(chunks, lambda c: far_copy(0, c).start())
    near_copy(0).start()
    each(chunks, lambda c: far_copy(1, c).start())
    near_copy(1).start()
    for k in range(3):
        s_copy(k).start()

    def start_w(i):
        w_copy(i, 0).start()
        w_copy(i, 1).start()

    def wait_w(i):
        w_copy(i, 0).wait()
        w_copy(i, 1).wait()

    each(RING, start_w)
    each(RING2, lambda j: w2_copy(j).start())

    def clear(e):
        acc[0, e] = jnp.zeros_like(acc[0, e])
        acc[1, e] = jnp.zeros_like(acc[1, e])
        gacc[e] = jnp.zeros_like(gacc[e])

    each(experts, clear)

    for k in range(3):
        s_copy(k).wait()
    at = dot(x[...], s1v[...]).astype(BF16).astype(F32).T
    bt = dot(x[...], s3v[...]).astype(BF16).astype(F32).T
    sht, sdat, sdbt = swiglu_parts(at, bt, dot_nt(s2v[...], dy[...]))
    sht_o[...], sdat_o[...], sdbt_o[...] = sht, sdat, sdbt

    def shared_back(m):
        own[span(m, COLS), :] = dot(s1v[span(m, COLS), :], sdat_o[...]) + dot(s3v[span(m, COLS), :], sdbt_o[...])

    each(chunks, shared_back)

    for k in range(3):
        tab_copy(k).wait()
    tg_o[...] = tg[...]
    make_picks((tab, tg.at[0], tg.at[1], tg.at[2]), first, pick, gate)
    for h in range(2):
        spread[h] = jnp.zeros_like(spread[h])
        for e in range(experts):
            for j in range(2):
                spread[h, e * 2 * SLOTS + j * SLOTS:e * 2 * SLOTS + (j + 1) * SLOTS, j * n:(j + 1) * n] = pick[2 * h + j, e * SLOTS:(e + 1) * SLOTS, :]

    def gather_chunk(a, c):
        far_copy(a, c).wait()
        hop_copy(a, c).start()
        for q in range(4):
            if q == 3:
                hop_copy(a, c).wait()
            src = own_of[a] if q == 0 else got_of[a].at[q - 1]
            got = dot(pick[q], src[:, span(c, COLS)])
            if a == 1:
                got = got * gate[q]
            put_rows(got.astype(BF16), q, rows)

    near_copy(0).wait()

    def up_chunk(c):
        gather_chunk(0, c)

        def up(e):
            i = c * experts + e
            wait_w(i)
            acc[0, e] += dot(rows[e], wring[i % RING, 0])
            acc[1, e] += dot(rows[e], wring[i % RING, 1])
            start_w(i + RING)

        each(experts, up)

    each(chunks, up_chunk)
    pltpu.make_async_copy(xg, xg_o, osem.at[0]).start()

    def turn(e):
        act[0, e] = acc[0, e].T.astype(BF16)
        act[1, e] = acc[1, e].T.astype(BF16)

    each(experts, turn)
    near_copy(1).wait()

    def down_chunk(c):
        gather_chunk(1, c)

        def down(e):
            j = c * experts + e
            w2_copy(j).wait()
            gacc[e] += dot_nt(w2ring[j % RING2], rows[e])

            @pl.when(j + RING2 < pieces)
            def _():
                w2_copy(j + RING2).start()

        each(experts, down)

    each(chunks, down_chunk)
    pltpu.make_async_copy(yg, yg_o, osem.at[1]).start()

    def middle(e):
        ht, dat, dbt = swiglu_parts(act[0, e], act[1, e], gacc[e])
        act[0, e], act[1, e], act[2, e] = dat, dbt, ht

    each(experts, middle)
    for k in range(3):
        pltpu.make_async_copy(act.at[k], (dat_o, dbt_o, ht_o)[k], osem.at[2 + k]).start()

    def back_chunk(m):
        def back(e):
            i = pieces + m * experts + e
            wait_w(i)
            part = (dot(wring[i % RING, 0], act[0, e]) + dot(wring[i % RING, 1], act[1, e])).astype(BF16)
            for h in range(2):
                ret[h, :, span(e, 2 * SLOTS)] = part[:, h * 2 * SLOTS:(h + 1) * 2 * SLOTS]

            @pl.when(i + RING < 2 * pieces)
            def _():
                start_w(i + RING)

        each(experts, back)
        sbuf[m] = dot(ret[1], spread[1])
        sum_copy(m).start()
        keep = dot(ret[0], spread[0])
        own[span(m, COLS), :] += keep[:, :n]
        far[span(m, COLS), :] = keep[:, n:]

    each(chunks, back_chunk)

    def add_mate(m):
        sum_copy(m).wait()
        own[span(m, COLS), :] += rbuf[m, :, :n]
        far[span(m, COLS), :] += rbuf[m, :, n:]

    each(chunks, add_mate)
    pltpu.make_async_copy(xg, xg_o, osem.at[0]).wait()
    pltpu.make_async_copy(yg, yg_o, osem.at[1]).wait()
    for k in range(3):
        pltpu.make_async_copy(act.at[k], (dat_o, dbt_o, ht_o)[k], osem.at[2 + k]).wait()


def exchange_call(x, dy, tab, w1, w3, w2, s1, s3, s2):
    experts, d, ff = w1.shape
    n = x.shape[0]
    chunks, rows = d // COLS, 4 * SLOTS
    vmem, hbm = pl.BlockSpec(memory_space=pltpu.VMEM), pl.BlockSpec(memory_space=pl.ANY)
    dma = pltpu.SemaphoreType.DMA
    return pl.pallas_call(
        exchange_kernel,
        in_specs=[vmem] * 3 + [hbm] * 6,
        out_specs=[hbm] * 5 + [vmem] * 6,
        out_shape=[jax.ShapeDtypeStruct((experts, ff, rows), BF16)] * 3 + [jax.ShapeDtypeStruct((3, n, d), BF16)] * 2 + [jax.ShapeDtypeStruct((3,) + tab.shape, F32)] + [jax.ShapeDtypeStruct((ff, n), BF16)] * 3 + [jax.ShapeDtypeStruct((d, n), F32)] * 2,
        scratch_shapes=[
            pltpu.VMEM((3, n, d), BF16), pltpu.VMEM((3, n, d), BF16), pltpu.VMEM((3,) + tab.shape, F32),
            pltpu.VMEM((RING, 2, COLS, ff), BF16), pltpu.VMEM((RING2, ff, COLS), BF16),
            pltpu.VMEM((d, ff), BF16), pltpu.VMEM((d, ff), BF16), pltpu.VMEM((ff, d), BF16),
            pltpu.VMEM((2, experts, rows, ff), F32), pltpu.VMEM((experts, ff, rows), F32), pltpu.VMEM((3, experts, ff, rows), BF16),
            pltpu.VMEM((experts, rows, COLS), BF16), pltpu.VMEM((4, experts * SLOTS, n), BF16), pltpu.VMEM((4, experts * SLOTS, 1), F32),
            pltpu.VMEM((2, COLS, experts * 2 * SLOTS), BF16), pltpu.VMEM((2, experts * 2 * SLOTS, 2 * n), BF16),
            pltpu.VMEM((chunks, COLS, 2 * n), F32), pltpu.VMEM((chunks, COLS, 2 * n), F32),
            dma((2,)), dma((2,)), dma((2, chunks)), dma((2, chunks)), dma((2, chunks)), dma((2, chunks)), dma((3,)), dma((3,)), dma((chunks,)), dma((chunks,)),
            dma((RING, 2)), dma((RING2,)), dma((3,)), dma((5,)),
        ],
        compiler_params=pltpu.CompilerParams(collective_id=0, has_side_effects=True, vmem_limit_bytes=67043328),
        cost_estimate=pl.CostEstimate(flops=12 * experts * rows * d * ff, bytes_accessed=96 * 2**20, transcendentals=0),
        name='exchange',
    )(x, dy, tab, w1, w3, w2, s1, s3, s2)


def weight_kernel(first, tab, tg, x, dy, xg, yg, dat, dbt, ht, sdat, sdbt, sht, dw1, dw3, dw2, ds1, ds3, ds2, rows, pick, gate):
    c, e = pl.program_id(0), pl.program_id(1)

    @pl.when((c == 0) & (e == 0))
    def _():
        make_picks((tab, tg.at[0], tg.at[1], tg.at[2]), first[0], pick, gate)

    @pl.when(e == 0)
    def _():
        for q in range(4):
            src_x, src_y = (x, dy) if q == 0 else (xg.at[q - 1], yg.at[q - 1])
            put_rows(dot(pick[q], src_x[:, span(c, COLS)]).astype(BF16), q, rows.at[0])
            put_rows((dot(pick[q], src_y[:, span(c, COLS)]) * gate[q]).astype(BF16), q, rows.at[1])
        ds1[0] = dot_tt(x[:, span(c, COLS)], sdat[...])
        ds3[0] = dot_tt(x[:, span(c, COLS)], sdbt[...])
        ds2[0] = dot(sht[...], dy[:, span(c, COLS)])

    dw1[0] = dot_tt(rows[0, e], dat[e])
    dw3[0] = dot_tt(rows[0, e], dbt[e])
    dw2[0] = dot(ht[e], rows[1, e])


def weight_call(first, tab, tg, x, dy, xg, yg, dat, dbt, ht, sdat, sdbt, sht):
    experts, ff, rows = dat.shape
    n, d = x.shape
    vmem = pl.BlockSpec(memory_space=pltpu.VMEM)
    tall = pl.BlockSpec((1, COLS, ff), lambda c, e: (e, c, 0))
    wide = pl.BlockSpec((1, ff, COLS), lambda c, e: (e, 0, c))
    tall_shared = pl.BlockSpec((1, COLS, ff), lambda c, e: (0, c, 0))
    wide_shared = pl.BlockSpec((1, ff, COLS), lambda c, e: (0, 0, c))
    return pl.pallas_call(
        weight_kernel,
        grid=(d // COLS, experts),
        in_specs=[pl.BlockSpec(memory_space=pltpu.SMEM)] + [vmem] * 12,
        out_specs=[tall, tall, wide, tall_shared, tall_shared, wide_shared],
        out_shape=[jax.ShapeDtypeStruct((experts, d, ff), F32)] * 2 + [jax.ShapeDtypeStruct((experts, ff, d), F32)] + [jax.ShapeDtypeStruct((1, d, ff), F32)] * 2 + [jax.ShapeDtypeStruct((1, ff, d), F32)],
        scratch_shapes=[pltpu.VMEM((2, experts, rows, COLS), BF16), pltpu.VMEM((4, experts * SLOTS, n), BF16), pltpu.VMEM((4, experts * SLOTS, 1), F32)],
        compiler_params=pltpu.CompilerParams(vmem_limit_bytes=56 * 2**20),
        cost_estimate=pl.CostEstimate(flops=6 * experts * rows * d * ff, bytes_accessed=124 * 2**20, transcendentals=0),
        name='weights',
    )(first, tab, tg, x, dy, xg, yg, dat, dbt, ht, sdat, sdbt, sht)


def final_kernel(own, back, out):
    out[...] = (own[...] + back[...]).T.astype(BF16)


def final_call(own, back):
    d, n = own.shape
    vmem = pl.BlockSpec(memory_space=pltpu.VMEM)
    return pl.pallas_call(
        final_kernel,
        in_specs=[vmem, vmem],
        out_specs=vmem,
        out_shape=jax.ShapeDtypeStruct((n, d), BF16),
        name='final',
    )(own, back)


def solution(mesh):
    token_spec = P(('dp', 'ep'), None)
    expert_spec = P('ep', None, None)
    whole_spec = P(None, None)
    grad_spec = P(('dp', 'ep'), None, None)
    group = mesh.shape['ep']

    def local_backward(x, dy, expert_ids, gate_vals, slot_pos, w1, w3, w2, s1, s3, s2):
        local = w1.shape[0]
        num_experts = local * group
        ids_t, slots_t, gates_t = expert_ids.T, slot_pos.T, gate_vals.T
        chosen = ids_t[:, None, :] == jnp.arange(num_experts, dtype=jnp.int32)[None, :, None]
        slot_tab = jnp.max(jnp.where(chosen, slots_t[:, None, :], -1), axis=0).astype(F32)
        gate_tab = jnp.sum(jnp.where(chosen, gates_t[:, None, :], 0.0), axis=0)
        tab = jnp.stack([slot_tab, gate_tab])
        first = (lax.axis_index('ep') * local).astype(jnp.int32).reshape(1)

        dat, dbt, ht, xg, yg, tg, sdat, sdbt, sht, own, far = exchange_call(x, dy, tab, w1, w3, w2, s1, s3, s2)
        back = lax.ppermute(far, 'ep', [(i, i ^ 2) for i in range(group)])
        dw1, dw3, dw2, ds1, ds3, ds2 = weight_call(first, tab, tg, x, dy, xg, yg, dat, dbt, ht, sdat, sdbt, sht)
        grad_x = final_call(own, back)
        return grad_x, dw1, dw3, dw2, ds1, ds3, ds2

    return jax.shard_map(local_backward, mesh=mesh, in_specs=(token_spec, token_spec, token_spec, token_spec, token_spec, expert_spec, expert_spec, expert_spec, whole_spec, whole_spec, whole_spec), out_specs=(token_spec, grad_spec, grad_spec, grad_spec, grad_spec, grad_spec, grad_spec), check_vma=False)
```

time: 469 us -> 132 us (0.28); the launches traced: 462 us -> 132 us
  matrix products: 177 us -> 0 us
  local copies, waits for them, and re-layouts: 144 us -> 0.98 us
  Pallas kernels: 0 us -> 128 us
  waiting for transfers between devices: 96.2 us -> 0.01 us
  other arithmetic: 26 us -> 2.11 us
  starting transfers between devices: 17.3 us -> 0.39 us
    dot_general x16 -> x0, matrix products: 177 us -> none  [the longest x1 26.8 us: local_backward(): jnp.einsum('erf,erd->efd', hidden, dz_exp, preferred_element_type=jnp.flo...]
    pallas_call x0 -> x3, Pallas kernels: none -> 128 us  [the longest x1 76.4 us: exchange_call(): pl.pallas_call(exchange_kernel, in_specs=[vmem] * 3 + [hbm] * 6, out_spec...]
    all_to_all x3 -> x0, waiting for transfers between devices: 96.2 us -> none  [the longest x1 63 us: local_backward(): x_exp = lax.all_to_all(send_x, 'ep', 0, 1, tiled=True)]
    gather x4 -> x0, local copies, waits for them, and re-layouts: 50.6 us -> none  [take_rows(): return jnp.take(rows, row_index, axis=0, mode='fill', fill_value=0)]
    all_to_all x3 -> x0, local copies, waits for them, and re-layouts: 33.2 us -> none  [the longest x1 11.1 us: local_backward(): dz_exp = lax.all_to_all(send_dz, 'ep', 0, 1, tiled=True)]
    reshape x6 -> x0, local copies, waits for them, and re-layouts: 28.1 us -> none  [the longest x1 9.4 us: local_backward(): lax.all_to_all(grad_exp, 'ep', 1, 0, tiled=True)]
    all_to_all x3 -> x0, starting transfers between devices: 17.3 us -> none  [the longest x1 5.86 us: local_backward(): dz_exp = lax.all_to_all(send_dz, 'ep', 0, 1, tiled=True)]
    convert_element_type x1 -> x0, local copies, waits for them, and re-layouts: 10.7 us -> none  [local_backward(): (jnp.einsum('erf,edf->erd', grad_gate, w_gate, preferred_element_type=jnp...]
  transfers between devices with their start and end apart: 3 -> 1, of which waited for: 3 -> 0; matrix products, arithmetic and copies ran while one was open for 38% -> 0% of each run, Pallas kernels for 0% -> 37%
where the time goes in v2:
time: 132 us
  Pallas kernels  128 us (97%)
  other arithmetic  2.11 us (2%)
    pallas_call x1, Pallas kernels, exchange_call(): pl.pallas_call(exchange_kernel, in_specs=[vmem] * 3 + [hbm] * 6, out_spec...  76.4 us
    pallas_call x1, Pallas kernels, weight_call(): pl.pallas_call(weight_kernel, grid=(d // COLS, experts), in_specs=[pl.Blo...  49 us
  transfers between devices with their start and end apart: 1, of which 0 were waited for; matrix products, arithmetic and copies ran while one was open for 0% of the time, Pallas kernels for 37%

profile of v2, /device:TPU:0, one launch (start us, length us, event | category | flops | bytes accessed | tf_op | source)
XLA Modules:
  0.0 132.0 jit_solution(4858835311777200969)
XLA Ops:
  0.6 0.7 select_reduce_fusion
  1.4 0.7 select_reduce_fusion.1
  2.1 0.6 pad_maximum_fusion.tab
  2.8 76.4 %exchange.1 = (bf16[8,512,256]{2,1,0:T(8,128)(2,1)}, bf16[8,512,256]{2,1,0:T(8,128)(2,1)}, bf16[8,512,256]{2,1,0:T(8,128)(2,1)}, bf16[3,128,2048]{2,1,0:T(8,128)...) custom-call(bf16[128,2048]{1,0:T(8,128)(2,1)} %x.3, ...), custom_call_target="tpu_custom_call" | custom-call | flops 25769803776 | bytes 100663296 | tf_op jit(solution)/shard_map/exchange/pallas_call | solution.py:266
  79.1 0.4 collective-permute-start
  79.5 49.0 %weights.1 = (f32[8,2048,512]{2,1,0:T(8,128)}, f32[8,2048,512]{2,1,0:T(8,128)}, f32[8,512,2048]{2,1,0:T(8,128)}, f32[1,2048,512]{2,1,0:T(8,128)}, f32[1,2048,512]{2,1,0:T(8,128)}, /*index=5*/f32[1,512,2048]{2,1,0:T(8,128)}) custom-call(s32[1]{0:T(128)} %bitcast.5.first, f32[2,32,128]{2,1,0:T(8,128)} %pad_maximum_fusion.tab, ...), custom_call_target="tpu_custom_call" | custom-call | flops 12884901888 | bytes 130023424 | tf_op jit(solution)/shard_map/weights/pallas_call | solution.py:318
  128.5 0.0 collective-permute-done.back
  128.5 0.0 copy-start
  128.5 1.0 copy-done
  129.5 2.5 %final.1 = bf16[128,2048]{1,0:T(8,128)(2,1)} custom-call(f32[2048,128]{1,0:T(8,128)} %get-tuple-element.24.own, f32[2048,128]{1,0:T(8,128)} %copy-done), custom_call_target="tpu_custom_call" | custom-call | tf_op jit(solution)/shard_map/final/pallas_call | solution.py:338
  (1 shorter events, 0.0 us)
Async XLA Ops:
  79.1 49.4 %collective-permute-start = (f32[2048,128]{1,0:T(8,128)}, f32[2048,128]{1,0:T(8,128)S(1)}, u32[]{:S(2)}, u32[]{:S(2)}) collective-permute-start(f32[2048,128]{1,0:T(8,128)} %get-tuple-element.25), channel_id=1, source_target_pairs={{0,2},{1,3},{2,0},{3,1},{4,6},{5,7},{6,4},{7,5}} | collective-permute-start | bytes 3145736 | tf_op jit(solution)/shard_map/ppermute | solution.py:365
  128.5 1.0 copy-start

commit v3 on v2

v3 whole, which is shorter than its diff:
```python
import jax
import jax.numpy as jnp
from jax import lax
from jax.experimental import pallas as pl
from jax.experimental.pallas import tpu as pltpu
from jax.sharding import PartitionSpec as P


F32, BF16 = jnp.float32, jnp.bfloat16
MESH = pl.DeviceIdType.MESH
SLOTS = 64
COLS = 512
RING, RING2 = 12, 8
UP, DOWN, BACK = 4, 4, 4


def dot(a, b):
    return jnp.dot(a, b, preferred_element_type=F32)


def dot_nt(a, b):
    return lax.dot_general(a, b, (((1,), (1,)), ((), ())), preferred_element_type=F32)


def dot_tt(a, b):
    return lax.dot_general(a, b, (((0,), (1,)), ((), ())), preferred_element_type=F32)


def span(index, size):
    return pl.ds(pl.multiple_of(index * size, size), size)


def swiglu_parts(a, b, g):
    a, b = a.astype(F32), b.astype(F32)
    sigma = jax.nn.sigmoid(a)
    silu = a * sigma
    hidden = (silu * b).astype(BF16)
    grad_a = (g * b * sigma * (1.0 + a * (1.0 - sigma))).astype(BF16)
    grad_b = (g * silu).astype(BF16)
    return hidden, grad_a, grad_b


def put_rows(got, q, rows):
    for e in range(rows.shape[0]):
        rows[e, span(q, SLOTS), :] = got[e * SLOTS:(e + 1) * SLOTS]


def exchange_kernel(x, dy, ids, slots, gates, w1, w3, w2, s1, s3, s2, dat_o, dbt_o, ht_o, tok_o, pick_o, gate_o, sdat_o, sdbt_o, sht_o, own, far,
                    xg, yg, idg, slotg, gateg, wring, w2ring, s1v, s3v, s2v, acc, gacc, act, rows, pick, gate, ret, spread, sbuf, rbuf,
                    near_s, near_r, far_s, far_r, hop_s, hop_r, tab_s, tab_r, sum_s, sum_r, wsem, w2sem, ssem, osem):
    me = lax.axis_index('ep')
    core = me % 2
    mate = me + 1 - 2 * core
    other = (me + 2) % 4
    diag = (mate + 2) % 4
    experts, d, ff = w1.shape
    n = x.shape[0]
    chunks = d // COLS
    pieces = chunks * experts

    barrier = pltpu.get_barrier_semaphore()
    for peer in (mate, other, diag):
        pl.semaphore_signal(barrier, inc=1, device_id={'ep': peer}, device_id_type=MESH)

    def w_copy(i, k):
        src = (w1, w3)[k].at[i % experts, span((i // experts) % chunks, COLS), :]
        return pltpu.make_async_copy(src, wring.at[i % RING, k], wsem.at[i % RING, k])

    def w2_copy(j):
        return pltpu.make_async_copy(w2.at[j % experts, :, span(j // experts, COLS)], w2ring.at[j % RING2], w2sem.at[j % RING2])

    def s_copy(k):
        return pltpu.make_async_copy((s1, s3, s2)[k], (s1v, s3v, s2v)[k], ssem.at[k])

    def each(count, body):
        def step(i, carry):
            body(i)
            return carry

        lax.fori_loop(0, count, step, 0)

    def start_w(i):
        w_copy(i, 0).start()
        w_copy(i, 1).start()

    def wait_w(i):
        w_copy(i, 0).wait()
        w_copy(i, 1).wait()

    for k in range(3):
        s_copy(k).start()
    each(RING, start_w)
    each(RING2, lambda j: w2_copy(j).start())

    def remote(src, dst, send, recv, peer):
        return pltpu.make_async_remote_copy(src_ref=src, dst_ref=dst, send_sem=send, recv_sem=recv, device_id={'ep': peer}, device_id_type=MESH)

    own_of, got_of = (x, dy), (xg, yg)

    def far_copy(a, c):
        return remote(own_of[a].at[:, span(c, COLS)], got_of[a].at[0, :, span(c, COLS)], far_s.at[a, c], far_r.at[a, c], other)

    def near_copy(a):
        return remote(own_of[a], got_of[a].at[1], near_s.at[a], near_r.at[a], mate)

    def hop_copy(a, c):
        return remote(got_of[a].at[0, :, span(c, COLS)], got_of[a].at[2, :, span(c, COLS)], hop_s.at[a, c], hop_r.at[a, c], mate)

    def tab_copy(t, k):
        return remote((ids, slots, gates)[t], (idg, slotg, gateg)[t].at[k], tab_s.at[t, k], tab_r.at[t, k], (other, mate, diag)[k])

    def sum_copy(m):
        return remote(sbuf.at[m], rbuf.at[m], sum_s.at[m], sum_r.at[m], mate)

    pl.semaphore_wait(barrier, 3)
    for t in range(3):
        for k in range(3):
            tab_copy(t, k).start()
    each(chunks, lambda c: far_copy(0, c).start())
    near_copy(0).start()
    each(chunks, lambda c: far_copy(1, c).start())
    near_copy(1).start()

    def clear(e):
        acc[0, e] = jnp.zeros_like(acc[0, e])
        acc[1, e] = jnp.zeros_like(acc[1, e])
        gacc[e] = jnp.zeros_like(gacc[e])

    each(experts, clear)
    for k in range(3):
        s_copy(k).wait()
    at = dot(x[...], s1v[...]).astype(BF16).astype(F32).T
    bt = dot(x[...], s3v[...]).astype(BF16).astype(F32).T
    sht, sdat, sdbt = swiglu_parts(at, bt, dot_nt(s2v[...], dy[...]))
    sht_o[...], sdat_o[...], sdbt_o[...] = sht, sdat, sdbt

    def shared_back(m):
        own[span(m, COLS), :] = dot(s1v[span(m, COLS), :], sdat_o[...]) + dot(s3v[span(m, COLS), :], sdbt_o[...])

    each(chunks, shared_back)

    for t in range(3):
        for k in range(3):
            tab_copy(t, k).wait()
    mine = me * experts + lax.broadcasted_iota(jnp.int32, (experts, n), 0)
    rank = lax.broadcasted_iota(jnp.int32, (SLOTS, n), 0)
    for q in range(4):
        idq, slotq, gateq = (ids, slots, gates) if q == 0 else (idg.at[q - 1], slotg.at[q - 1], gateg.at[q - 1])
        slot = jnp.full((experts, n), -1, jnp.int32)
        weight = jnp.zeros((experts, n), F32)
        for j in range(ids.shape[0]):
            hit = mine == idq[j:j + 1, :]
            slot = jnp.where(hit, slotq[j:j + 1, :], slot)
            weight = jnp.where(hit, gateq[j:j + 1, :], weight)
        for e in range(experts):
            hit = rank == slot[e:e + 1, :]
            pick[q, e * SLOTS:(e + 1) * SLOTS, :] = jnp.where(hit, 1.0, 0.0).astype(BF16)
            gate[q, e * SLOTS:(e + 1) * SLOTS, :] = jnp.sum(jnp.where(hit, weight[e:e + 1, :], 0.0), axis=1, keepdims=True)
    for h in range(2):
        spread[h] = jnp.zeros_like(spread[h])
        for e in range(experts):
            for j in range(2):
                spread[h, e * 2 * SLOTS + j * SLOTS:e * 2 * SLOTS + (j + 1) * SLOTS, j * n:(j + 1) * n] = pick[2 * h + j, e * SLOTS:(e + 1) * SLOTS, :]

    def expect(a, c):
        far_copy(a, c).wait()
        hop_copy(a, c).start()

    def gather_chunk(a, c):
        hop_copy(a, c).wait()
        for q in range(4):
            src = own_of[a] if q == 0 else got_of[a].at[q - 1]
            got = dot(pick[q], src[:, span(c, COLS)])
            if a == 1:
                got = got * gate[q]
            put_rows(got.astype(BF16), q, rows)

    expect(0, 0)
    near_copy(0).wait()

    def up_chunk(c):
        gather_chunk(0, c)

        def up(p):
            base = c * experts + UP * p
            for k in range(UP):
                wait_w(base + k)
            for k in range(UP):
                e, i = UP * p + k, base + k
                acc[0, e] += dot(rows[e], wring[i % RING, 0])
                acc[1, e] += dot(rows[e], wring[i % RING, 1])
            for k in range(UP):
                start_w(base + k + RING)

        each(experts // UP // 2, up)

        @pl.when(c + 1 < chunks)
        def _():
            expect(0, c + 1)

        @pl.when(c + 1 == chunks)
        def _():
            expect(1, 0)

        each(experts // UP // 2, lambda p: up(p + experts // UP // 2))

    each(chunks, up_chunk)
    near_copy(1).wait()

    def down_chunk(c):
        gather_chunk(1, c)

        def down(p):
            base = c * experts + DOWN * p
            for k in range(DOWN):
                w2_copy(base + k).wait()
            parts = [dot_nt(w2ring[(base + k) % RING2], rows[DOWN * p + k]) for k in range(DOWN)]
            for k in range(DOWN):
                gacc[DOWN * p + k] += parts[k]

            @pl.when(base + RING2 < pieces)
            def _():
                for k in range(DOWN):
                    w2_copy(base + k + RING2).start()

        down(0)

        @pl.when(c + 1 < chunks)
        def _():
            expect(1, c + 1)

        each(experts // DOWN - 1, lambda p: down(p + 1))

    each(chunks, down_chunk)
    outs = [pltpu.make_async_copy(x, tok_o.at[0, 0], osem.at[0]), pltpu.make_async_copy(xg, tok_o.at[0, 1:4], osem.at[1]),
            pltpu.make_async_copy(dy, tok_o.at[1, 0], osem.at[2]), pltpu.make_async_copy(yg, tok_o.at[1, 1:4], osem.at[3]),
            pltpu.make_async_copy(pick, pick_o, osem.at[4]), pltpu.make_async_copy(gate, gate_o, osem.at[5])]
    for copy in outs:
        copy.start()

    half = ff // 2

    def middle(i):
        e, part = i // 2, span(i % 2, half)
        a, b = acc[0, e, :, part].T.astype(BF16), acc[1, e, :, part].T.astype(BF16)
        act[2, e, part, :], act[0, e, part, :], act[1, e, part, :] = swiglu_parts(a, b, gacc[e, part, :])

    each(2 * experts, middle)
    outs += [pltpu.make_async_copy(act.at[k], (dat_o, dbt_o, ht_o)[k], osem.at[6 + k]) for k in range(3)]
    for copy in outs[6:]:
        copy.start()

    def back_chunk(m):
        def back(p):
            base = pieces + m * experts + BACK * p
            for k in range(BACK):
                wait_w(base + k)
            for k in range(BACK):
                e, i = BACK * p + k, base + k
                part = (dot(wring[i % RING, 0], act[0, e]) + dot(wring[i % RING, 1], act[1, e])).astype(BF16)
                for h in range(2):
                    ret[h, :, span(e, 2 * SLOTS)] = part[:, h * 2 * SLOTS:(h + 1) * 2 * SLOTS]

            @pl.when(base + RING < 2 * pieces)
            def _():
                for k in range(BACK):
                    start_w(base + k + RING)

        each(experts // BACK, back)
        give = dot(ret[1], spread[1])
        keep = dot(ret[0], spread[0])
        sbuf[m] = give
        own[span(m, COLS), :] += keep[:, :n]
        far[span(m, COLS), :] = keep[:, n:]
        sum_copy(m).start()

    each(chunks, back_chunk)

    def add_mate(m):
        sum_copy(m).wait()
        own[span(m, COLS), :] += rbuf[m, :, :n]
        far[span(m, COLS), :] += rbuf[m, :, n:]

    each(chunks, add_mate)
    for copy in outs:
        copy.wait()


def exchange_call(x, dy, ids, slots, gates, w1, w3, w2, s1, s3, s2):
    experts, d, ff = w1.shape
    n = x.shape[0]
    chunks, rows = d // COLS, 4 * SLOTS
    vmem, hbm = pl.BlockSpec(memory_space=pltpu.VMEM), pl.BlockSpec(memory_space=pl.ANY)
    dma = pltpu.SemaphoreType.DMA
    return pl.pallas_call(
        exchange_kernel,
        in_specs=[vmem] * 5 + [hbm] * 6,
        out_specs=[hbm] * 6 + [vmem] * 5,
        out_shape=[jax.ShapeDtypeStruct((experts, ff, rows), BF16)] * 3 + [jax.ShapeDtypeStruct((2, 4, n, d), BF16), jax.ShapeDtypeStruct((4, experts * SLOTS, n), BF16), jax.ShapeDtypeStruct((4, experts * SLOTS, 1), F32)] + [jax.ShapeDtypeStruct((ff, n), BF16)] * 3 + [jax.ShapeDtypeStruct((d, n), F32)] * 2,
        scratch_shapes=[
            pltpu.VMEM((3, n, d), BF16), pltpu.VMEM((3, n, d), BF16), pltpu.VMEM((3,) + ids.shape, jnp.int32), pltpu.VMEM((3,) + ids.shape, jnp.int32), pltpu.VMEM((3,) + ids.shape, F32),
            pltpu.VMEM((RING, 2, COLS, ff), BF16), pltpu.VMEM((RING2, ff, COLS), BF16),
            pltpu.VMEM((d, ff), BF16), pltpu.VMEM((d, ff), BF16), pltpu.VMEM((ff, d), BF16),
            pltpu.VMEM((2, experts, rows, ff), F32), pltpu.VMEM((experts, ff, rows), F32), pltpu.VMEM((3, experts, ff, rows), BF16),
            pltpu.VMEM((experts, rows, COLS), BF16), pltpu.VMEM((4, experts * SLOTS, n), BF16), pltpu.VMEM((4, experts * SLOTS, 1), F32),
            pltpu.VMEM((2, COLS, experts * 2 * SLOTS), BF16), pltpu.VMEM((2, experts * 2 * SLOTS, 2 * n), BF16),
            pltpu.VMEM((chunks, COLS, 2 * n), F32), pltpu.VMEM((chunks, COLS, 2 * n), F32),
            dma((2,)), dma((2,)), dma((2, chunks)), dma((2, chunks)), dma((2, chunks)), dma((2, chunks)), dma((3, 3)), dma((3, 3)), dma((chunks,)), dma((chunks,)),
            dma((RING, 2)), dma((RING2,)), dma((3,)), dma((9,)),
        ],
        compiler_params=pltpu.CompilerParams(collective_id=0, has_side_effects=True, vmem_limit_bytes=67043328),
        cost_estimate=pl.CostEstimate(flops=12 * experts * rows * d * ff, bytes_accessed=96 * 2**20, transcendentals=0),
        name='exchange',
    )(x, dy, ids, slots, gates, w1, w3, w2, s1, s3, s2)


def weight_kernel(tok, pick, gate, dat_h, dbt_h, ht_h, sdat, sdbt, sht, dw1, dw3, dw2, ds1, ds3, ds2, rows, act, sem):
    c, e = pl.program_id(0), pl.program_id(1)
    chunks, experts = pl.num_programs(0), rows.shape[2]
    now, later = c % 2, (c + 1) % 2

    def act_copy(k, i):
        return pltpu.make_async_copy((dat_h, dbt_h, ht_h)[k].at[i], act.at[k, i], sem.at[k, i])

    def put(a, q, col, buf):
        got = dot(pick[q], tok[a, q, :, span(col, COLS)])
        if isinstance(a, int):
            got = got * gate[q] if a == 1 else got
        else:
            got = got * jnp.where(a == 1, gate[q], 1.0)
        put_rows(got.astype(BF16), q, rows.at[buf, a])

    @pl.when((c == 0) & (e == 0))
    def _():
        for i in range(experts):
            for k in range(3):
                act_copy(k, i).start()
        for q in range(4):
            put(0, q, 0, 0)
            put(1, q, 0, 0)

    @pl.when(c == 0)
    def _():
        for k in range(3):
            act_copy(k, e).wait()

    @pl.when(e == 0)
    def _():
        ds1[0] = dot_tt(tok[0, 0, :, span(c, COLS)], sdat[...])
        ds3[0] = dot_tt(tok[0, 0, :, span(c, COLS)], sdbt[...])
        ds2[0] = dot(sht[...], tok[1, 0, :, span(c, COLS)])

    @pl.when(c + 1 < chunks)
    def _():
        put(e % 2, e // 2, c + 1, later)

    xt = rows[now, 0, e].T
    dw1[0] = dot_nt(xt, act[0, e])
    dw3[0] = dot_nt(xt, act[1, e])
    dw2[0] = dot(act[2, e], rows[now, 1, e])


def weight_call(tok, pick, gate, dat, dbt, ht, sdat, sdbt, sht):
    experts, ff, rows = dat.shape
    _, d = tok.shape[2:]
    vmem, hbm = pl.BlockSpec(memory_space=pltpu.VMEM), pl.BlockSpec(memory_space=pl.ANY)
    tall = pl.BlockSpec((1, COLS, ff), lambda c, e: (e, c, 0))
    wide = pl.BlockSpec((1, ff, COLS), lambda c, e: (e, 0, c))
    tall_shared = pl.BlockSpec((1, COLS, ff), lambda c, e: (0, c, 0))
    wide_shared = pl.BlockSpec((1, ff, COLS), lambda c, e: (0, 0, c))
    return pl.pallas_call(
        weight_kernel,
        grid=(d // COLS, experts),
        in_specs=[vmem] * 3 + [hbm] * 3 + [vmem] * 3,
        out_specs=[tall, tall, wide, tall_shared, tall_shared, wide_shared],
        out_shape=[jax.ShapeDtypeStruct((experts, d, ff), F32)] * 2 + [jax.ShapeDtypeStruct((experts, ff, d), F32)] + [jax.ShapeDtypeStruct((1, d, ff), F32)] * 2 + [jax.ShapeDtypeStruct((1, ff, d), F32)],
        scratch_shapes=[pltpu.VMEM((2, 2, experts, rows, COLS), BF16), pltpu.VMEM((3, experts, ff, rows), BF16), pltpu.SemaphoreType.DMA((3, experts))],
        compiler_params=pltpu.CompilerParams(vmem_limit_bytes=56 * 2**20),
        cost_estimate=pl.CostEstimate(flops=6 * experts * rows * d * ff, bytes_accessed=124 * 2**20, transcendentals=0),
        name='weights',
    )(tok, pick, gate, dat, dbt, ht, sdat, sdbt, sht)


def final_kernel(own, back, out):
    out[...] = (own[...] + back[...]).T.astype(BF16)


def final_call(own, back):
    d, n = own.shape
    vmem = pl.BlockSpec(memory_space=pltpu.VMEM)
    return pl.pallas_call(
        final_kernel,
        in_specs=[vmem, vmem],
        out_specs=vmem,
        out_shape=jax.ShapeDtypeStruct((n, d), BF16),
        name='final',
    )(own, back)


def solution(mesh):
    token_spec = P(('dp', 'ep'), None)
    expert_spec = P('ep', None, None)
    whole_spec = P(None, None)
    grad_spec = P(('dp', 'ep'), None, None)
    group = mesh.shape['ep']

    def local_backward(x, dy, expert_ids, gate_vals, slot_pos, w1, w3, w2, s1, s3, s2):
        dat, dbt, ht, tok, pick, gate, sdat, sdbt, sht, own, far = exchange_call(x, dy, expert_ids.T, slot_pos.T, gate_vals.T, w1, w3, w2, s1, s3, s2)
        back = lax.ppermute(far, 'ep', [(i, i ^ 2) for i in range(group)])
        dw1, dw3, dw2, ds1, ds3, ds2 = weight_call(tok, pick, gate, dat, dbt, ht, sdat, sdbt, sht)
        grad_x = final_call(own, back)
        return grad_x, dw1, dw3, dw2, ds1, ds3, ds2

    return jax.shard_map(local_backward, mesh=mesh, in_specs=(token_spec, token_spec, token_spec, token_spec, token_spec, expert_spec, expert_spec, expert_spec, whole_spec, whole_spec, whole_spec), out_specs=(token_spec, grad_spec, grad_spec, grad_spec, grad_spec, grad_spec, grad_spec), check_vma=False)
```

time: 132 us -> 109 us (0.83)
  Pallas kernels: 128 us -> 106 us
  other arithmetic: 2.11 us -> 0 us
  starting transfers between devices: 0.39 us -> 1.79 us
    pallas_call x2, Pallas kernels: 125 us -> 103 us  [the longest x1 57 us: exchange_call(): pl.pallas_call(exchange_kernel, in_specs=[vmem] * 5 + [hbm] * 6, out_spec...]
    ppermute x1, starting transfers between devices: 0.39 us -> 1.79 us  [local_backward(): back = lax.ppermute(far, 'ep', [(i, i ^ 2) for i in range(group)])]
  transfers between devices with their start and end apart: 1 -> 1, of which waited for: 0 -> 0; matrix products, arithmetic and copies ran while one was open for 0% -> 0% of each run, Pallas kernels for 37% -> 42%
where the time goes in v3:
time: 109 us
  Pallas kernels  106 us (97%)
  starting transfers between devices  1.79 us (2%)
    pallas_call x1, Pallas kernels, exchange_call(): pl.pallas_call(exchange_kernel, in_specs=[vmem] * 5 + [hbm] * 6, out_spec...  57 us
    pallas_call x1, Pallas kernels, weight_call(): pl.pallas_call(weight_kernel, grid=(d // COLS, experts), in_specs=[vmem]...  46.3 us
    pallas_call x1, Pallas kernels, final_call(): pl.pallas_call(final_kernel, in_specs=[vmem, vmem], out_specs=vmem, out_s...  2.54 us
  transfers between devices with their start and end apart: 1, of which 0 were waited for; matrix products, arithmetic and copies ran while one was open for 0% of the time, Pallas kernels for 42%

profile of v3, /device:TPU:0, one launch (start us, length us, event | category | flops | bytes accessed | tf_op | source)
XLA Modules:
  0.0 109.3 jit_solution(8439441745635028409)
XLA Ops:
  0.6 57.0 %exchange.1 = (bf16[8,512,256]{2,1,0:T(8,128)(2,1)}, bf16[8,512,256]{2,1,0:T(8,128)(2,1)}, bf16[8,512,256]{2,1,0:T(8,128)(2,1)}, bf16[2,4,128,2048]{3,2,1,0:T(8,...) custom-call(bf16[128,2048]{1,0:T(8,128)(2,1)} %x.1, ...), custom_call_target="tpu_custom_call" | custom-call | flops 25769803776 | bytes 100663296 | tf_op jit(solution)/shard_map/exchange/pallas_call | solution.py:295
  57.6 1.8 %collective-permute-start = (f32[2048,128]{1,0:T(8,128)}, f32[2048,128]{1,0:T(8,128)S(1)}, u32[]{:S(2)}, u32[]{:S(2)}) collective-permute-start(f32[2048,128]{1,0:T(8,128)} %get-tuple-element.25), channel_id=1, source_target_pairs={{0,2},{1,3},{2,0},{3,1},{4,6},{5,7},{6,4},{7,5}} | collective-permute-start | bytes 3145736 | tf_op jit(solution)/shard_map/ppermute | solution.py:409
  59.4 46.3 %weights.1 = (f32[8,2048,512]{2,1,0:T(8,128)}, f32[8,2048,512]{2,1,0:T(8,128)}, f32[8,512,2048]{2,1,0:T(8,128)}, f32[1,2048,512]{2,1,0:T(8,128)}, f32[1,2048,512]{2,1,0:T(8,128)}, /*index=5*/f32[1,512,2048]{2,1,0:T(8,128)}) custom-call(bf16[2,4,128,2048]{3,2,1,0:T(8,128)(2,1)} %get-tuple-element.26.tok, bf16[4,512,128]{2,1,0:T(8,128)(2,1)} %get-tuple-element.27.pick, ...), custom_call_target="tpu_custom_call" | custom-call | flops 12884901888 | bytes 130023424 | tf_op jit(solution)/shard_map/weights/pallas_call | solution.py:371
  105.7 0.0 collective-permute-done.back
  105.7 0.0 copy-start
  105.8 1.0 copy-done
  106.7 2.5 %final.1 = bf16[128,2048]{1,0:T(8,128)(2,1)} custom-call(f32[2048,128]{1,0:T(8,128)} %get-tuple-element.24.own, f32[2048,128]{1,0:T(8,128)} %copy-done), custom_call_target="tpu_custom_call" | custom-call | tf_op jit(solution)/shard_map/final/pallas_call | solution.py:391
Async XLA Ops:
  57.6 48.1 %collective-permute-start = (f32[2048,128]{1,0:T(8,128)}, f32[2048,128]{1,0:T(8,128)S(1)}, u32[]{:S(2)}, u32[]{:S(2)}) collective-permute-start(f32[2048,128]{1,0:T(8,128)} %get-tuple-element.25), channel_id=1, source_target_pairs={{0,2},{1,3},{2,0},{3,1},{4,6},{5,7},{6,4},{7,5}} | collective-permute-start | bytes 3145736 | tf_op jit(solution)/shard_map/ppermute | solution.py:409
  105.7 1.0 copy-start

commit v4 on v3

--- a/solution.py
+++ b/solution.py
@@ -11,6 +11,7 @@
 SLOTS = 64
 COLS = 512
 RING, RING2 = 12, 8
+OUTS = 5
 UP, DOWN, BACK = 4, 4, 4
 
 
@@ -22,20 +23,16 @@
     return lax.dot_general(a, b, (((1,), (1,)), ((), ())), preferred_element_type=F32)
 
 
-def dot_tt(a, b):
-    return lax.dot_general(a, b, (((0,), (1,)), ((), ())), preferred_element_type=F32)
-
-
 def span(index, size):
     return pl.ds(pl.multiple_of(index * size, size), size)
 
 
 def swiglu_parts(a, b, g):
     a, b = a.astype(F32), b.astype(F32)
-    sigma = jax.nn.sigmoid(a)
+    sigma = 0.5 * jnp.tanh(0.5 * a) + 0.5
     silu = a * sigma
     hidden = (silu * b).astype(BF16)
-    grad_a = (g * b * sigma * (1.0 + a * (1.0 - sigma))).astype(BF16)
+    grad_a = (g * b * (sigma + silu * (1.0 - sigma))).astype(BF16)
     grad_b = (g * silu).astype(BF16)
     return hidden, grad_a, grad_b
 
@@ -118,7 +115,6 @@
             tab_copy(t, k).start()
     each(chunks, lambda c: far_copy(0, c).start())
     near_copy(0).start()
-    each(chunks, lambda c: far_copy(1, c).start())
     near_copy(1).start()
 
     def clear(e):
@@ -179,6 +175,7 @@
     near_copy(0).wait()
 
     def up_chunk(c):
+        far_copy(1, c).start()
         gather_chunk(0, c)
 
         def up(p):
@@ -314,85 +311,157 @@
     )(x, dy, ids, slots, gates, w1, w3, w2, s1, s3, s2)
 
 
-def weight_kernel(tok, pick, gate, dat_h, dbt_h, ht_h, sdat, sdbt, sht, dw1, dw3, dw2, ds1, ds3, ds2, rows, act, sem):
-    c, e = pl.program_id(0), pl.program_id(1)
-    chunks, experts = pl.num_programs(0), rows.shape[2]
-    now, later = c % 2, (c + 1) % 2
+def weight_kernel(sdat, sdbt, sht, tok_h, pick_h, gate_h, dat_h, dbt_h, ht_h, dw1, dw3, dw2, ds1, ds3, ds2, tok, pick, gate, act, rows, obuf, tsem, asem, osem):
+    experts, d, _ = dw1.shape
+    chunks = d // COLS
+    slots = obuf.shape[0]
+
+    def each(start, stop, body):
+        def step(i, carry):
+            body(i)
+            return carry
+
+        lax.fori_loop(start, stop, step, 0)
+
+    def tok_copy(c):
+        return pltpu.make_async_copy(tok_h.at[:, :, :, span(c, COLS)], tok.at[:, :, :, span(c, COLS)], tsem.at[c])
 
     def act_copy(k, i):
-        return pltpu.make_async_copy((dat_h, dbt_h, ht_h)[k].at[i], act.at[k, i], sem.at[k, i])
-
-    def put(a, q, col, buf):
-        got = dot(pick[q], tok[a, q, :, span(col, COLS)])
-        if isinstance(a, int):
-            got = got * gate[q] if a == 1 else got
-        else:
-            got = got * jnp.where(a == 1, gate[q], 1.0)
-        put_rows(got.astype(BF16), q, rows.at[buf, a])
-
-    @pl.when((c == 0) & (e == 0))
-    def _():
-        for i in range(experts):
+        return pltpu.make_async_copy((dat_h, dbt_h, ht_h)[k].at[i], act.at[k, i], asem.at[k, i])
+
+    def out_copy(refs, k, i, c, slot):
+        dst = refs[k].at[i, :, span(c, COLS)] if k == 2 else refs[k].at[i, span(c, COLS), :]
+        return pltpu.make_async_copy(obuf.at[slot, k], dst, osem.at[slot, k])
+
+    pick_copy = pltpu.make_async_copy(pick_h, pick, tsem.at[chunks])
+    gate_copy = pltpu.make_async_copy(gate_h, gate, tsem.at[chunks + 1])
+    tok_copy(0).start()
+    pick_copy.start()
+    gate_copy.start()
+    each(1, chunks, lambda c: tok_copy(c).start())
+
+    def start_act(i):
+        for k in range(3):
+            act_copy(k, i).start()
+
+    each(0, experts, start_act)
+
+    routed, shared = (dw1, dw3, dw2), (ds1, ds3, ds2)
+
+    def claim(t):
+        @pl.when(t >= slots)
+        def _():
             for k in range(3):
-                act_copy(k, i).start()
-        for q in range(4):
-            put(0, q, 0, 0)
-            put(1, q, 0, 0)
-
-    @pl.when(c == 0)
-    def _():
+                out_copy(routed, k, 0, 0, t % slots).wait()
+
+    def shared_item(c):
+        t = c * (experts + 1)
+        claim(t)
+        slot = t % slots
+        xt = tok[0, 0, :, span(c, COLS)].T
+        obuf[slot, 0] = dot_nt(xt, sdat[...])
+        obuf[slot, 1] = dot_nt(xt, sdbt[...])
+        obuf[slot, 2] = dot(sht[...], tok[1, 0, :, span(c, COLS)])
         for k in range(3):
-            act_copy(k, e).wait()
-
-    @pl.when(e == 0)
-    def _():
-        ds1[0] = dot_tt(tok[0, 0, :, span(c, COLS)], sdat[...])
-        ds3[0] = dot_tt(tok[0, 0, :, span(c, COLS)], sdbt[...])
-        ds2[0] = dot(sht[...], tok[1, 0, :, span(c, COLS)])
-
-    @pl.when(c + 1 < chunks)
-    def _():
-        put(e % 2, e // 2, c + 1, later)
-
-    xt = rows[now, 0, e].T
-    dw1[0] = dot_nt(xt, act[0, e])
-    dw3[0] = dot_nt(xt, act[1, e])
-    dw2[0] = dot(act[2, e], rows[now, 1, e])
+            out_copy(shared, k, 0, c, slot).start()
+
+    tok_copy(0).wait()
+    shared_item(0)
+    pick_copy.wait()
+    gate_copy.wait()
+    for q in range(4):
+        put_rows(dot(pick[q], tok[0, q, :, :COLS]).astype(BF16), q, rows.at[0, 0])
+        put_rows((dot(pick[q], tok[1, q, :, :COLS]) * gate[q]).astype(BF16), q, rows.at[0, 1])
+
+    def chunk(c):
+        now, later, follow = c % 2, (c + 1) % 2, (c + 1) % chunks
+
+        @pl.when(c > 0)
+        def _():
+            shared_item(c)
+
+        @pl.when(c + 1 < chunks)
+        def _():
+            tok_copy(c + 1).wait()
+
+        def expert(e):
+            t = c * (experts + 1) + 1 + e
+            claim(t)
+
+            @pl.when(c == 0)
+            def _():
+                for k in range(3):
+                    act_copy(k, e).wait()
+
+            slot = t % slots
+            a, q = e % 2, e // 2
+            got = dot(pick[q], tok[a, q, :, span(follow, COLS)]) * jnp.where(a == 1, gate[q], 1.0)
+            xt = rows[now, 0, e].T
+            obuf[slot, 0] = dot_nt(xt, act[0, e])
+            obuf[slot, 1] = dot_nt(xt, act[1, e])
+            obuf[slot, 2] = dot(act[2, e], rows[now, 1, e])
+            put_rows(got.astype(BF16), q, rows.at[later, a])
+            for k in range(3):
+                out_copy(routed, k, e, c, slot).start()
+
+        each(0, experts, expert)
+
+    each(0, chunks, chunk)
+    for slot in range(slots):
+        for k in range(3):
+            out_copy(routed, k, 0, 0, slot).wait()
 
 
 def weight_call(tok, pick, gate, dat, dbt, ht, sdat, sdbt, sht):
     experts, ff, rows = dat.shape
     _, d = tok.shape[2:]
+    chunks = d // COLS
     vmem, hbm = pl.BlockSpec(memory_space=pltpu.VMEM), pl.BlockSpec(memory_space=pl.ANY)
-    tall = pl.BlockSpec((1, COLS, ff), lambda c, e: (e, c, 0))
-    wide = pl.BlockSpec((1, ff, COLS), lambda c, e: (e, 0, c))
-    tall_shared = pl.BlockSpec((1, COLS, ff), lambda c, e: (0, c, 0))
-    wide_shared = pl.BlockSpec((1, ff, COLS), lambda c, e: (0, 0, c))
+    dma = pltpu.SemaphoreType.DMA
     return pl.pallas_call(
         weight_kernel,
-        grid=(d // COLS, experts),
-        in_specs=[vmem] * 3 + [hbm] * 3 + [vmem] * 3,
-        out_specs=[tall, tall, wide, tall_shared, tall_shared, wide_shared],
+        in_specs=[vmem] * 3 + [hbm] * 6,
+        out_specs=[hbm] * 6,
         out_shape=[jax.ShapeDtypeStruct((experts, d, ff), F32)] * 2 + [jax.ShapeDtypeStruct((experts, ff, d), F32)] + [jax.ShapeDtypeStruct((1, d, ff), F32)] * 2 + [jax.ShapeDtypeStruct((1, ff, d), F32)],
-        scratch_shapes=[pltpu.VMEM((2, 2, experts, rows, COLS), BF16), pltpu.VMEM((3, experts, ff, rows), BF16), pltpu.SemaphoreType.DMA((3, experts))],
-        compiler_params=pltpu.CompilerParams(vmem_limit_bytes=56 * 2**20),
+        scratch_shapes=[
+            pltpu.VMEM(tok.shape, BF16), pltpu.VMEM(pick.shape, BF16), pltpu.VMEM(gate.shape, F32), pltpu.VMEM((3, experts, ff, rows), BF16),
+            pltpu.VMEM((2, 2, experts, rows, COLS), BF16), pltpu.VMEM((OUTS, 3, COLS, ff), F32),
+            dma((chunks + 2,)), dma((3, experts)), dma((OUTS, 3)),
+        ],
+        compiler_params=pltpu.CompilerParams(vmem_limit_bytes=60 * 2**20),
         cost_estimate=pl.CostEstimate(flops=6 * experts * rows * d * ff, bytes_accessed=124 * 2**20, transcendentals=0),
         name='weights',
-    )(tok, pick, gate, dat, dbt, ht, sdat, sdbt, sht)
-
-
-def final_kernel(own, back, out):
-    out[...] = (own[...] + back[...]).T.astype(BF16)
+    )(sdat, sdbt, sht, tok, pick, gate, dat, dbt, ht)
+
+
+def final_kernel(own_h, back_h, out_h, own, back, out, isem, osem):
+    parts = own.shape[0] // COLS
+    loads = [[pltpu.make_async_copy(src.at[pl.ds(p * COLS, COLS), :], dst.at[pl.ds(p * COLS, COLS), :], isem.at[k, p]) for k, (src, dst) in enumerate(((own_h, own), (back_h, back)))] for p in range(parts)]
+    for pair in loads:
+        for copy in pair:
+            copy.start()
+    stores = []
+    for p in range(parts):
+        for copy in loads[p]:
+            copy.wait()
+        at = pl.ds(p * COLS, COLS)
+        out[:, at] = (own[at, :] + back[at, :]).T.astype(BF16)
+        stores.append(pltpu.make_async_copy(out.at[:, at], out_h.at[:, at], osem.at[p]))
+        stores[-1].start()
+    for copy in stores:
+        copy.wait()
 
 
 def final_call(own, back):
     d, n = own.shape
-    vmem = pl.BlockSpec(memory_space=pltpu.VMEM)
+    hbm = pl.BlockSpec(memory_space=pl.ANY)
     return pl.pallas_call(
         final_kernel,
-        in_specs=[vmem, vmem],
-        out_specs=vmem,
+        in_specs=[hbm, hbm],
+        out_specs=hbm,
         out_shape=jax.ShapeDtypeStruct((n, d), BF16),
+        scratch_shapes=[pltpu.VMEM((d, n), F32), pltpu.VMEM((d, n), F32), pltpu.VMEM((n, d), BF16), pltpu.SemaphoreType.DMA((2, d // COLS)), pltpu.SemaphoreType.DMA((d // COLS,))],
+        compiler_params=pltpu.CompilerParams(vmem_limit_bytes=67043328),
         name='final',
     )(own, back)
 

time: 109 us -> 101 us (0.927)
  Pallas kernels: 106 us -> 98.9 us
    pallas_call x2, Pallas kernels: 48.8 us -> 41.9 us  [the longest x1 39.5 us: weight_call(): pl.pallas_call(weight_kernel, in_specs=[vmem] * 3 + [hbm] * 6, out_specs=...]
  transfers between devices with their start and end apart: 1 -> 1, of which waited for: 0 -> 0; matrix products, arithmetic and copies ran while one was open for 0% -> 0% of each run, Pallas kernels for 42% -> 39%
where the time goes in v4:
time: 101 us
  Pallas kernels  98.9 us (98%)
  starting transfers between devices  1.78 us (2%)
    pallas_call x1, Pallas kernels, exchange_call(): pl.pallas_call(exchange_kernel, in_specs=[vmem] * 5 + [hbm] * 6, out_spec...  57 us
    pallas_call x1, Pallas kernels, weight_call(): pl.pallas_call(weight_kernel, in_specs=[vmem] * 3 + [hbm] * 6, out_specs=...  39.5 us
    pallas_call x1, Pallas kernels, final_call(): pl.pallas_call(final_kernel, in_specs=[hbm, hbm], out_specs=hbm, out_shap...  2.37 us
  transfers between devices with their start and end apart: 1, of which 0 were waited for; matrix products, arithmetic and copies ran while one was open for 0% of the time, Pallas kernels for 39%

profile of v4, /device:TPU:0, one launch (start us, length us, event | category | flops | bytes accessed | tf_op | source)
XLA Modules:
  0.0 101.3 jit_solution(2964787164984099099)
XLA Ops:
  0.6 57.0 %exchange.1 = (bf16[8,512,256]{2,1,0:T(8,128)(2,1)}, bf16[8,512,256]{2,1,0:T(8,128)(2,1)}, bf16[8,512,256]{2,1,0:T(8,128)(2,1)}, bf16[2,4,128,2048]{3,2,1,0:T(8,...) custom-call(bf16[128,2048]{1,0:T(8,128)(2,1)} %x.1, ...), custom_call_target="tpu_custom_call" | custom-call | flops 25769803776 | bytes 100663296 | tf_op jit(solution)/shard_map/exchange/pallas_call | solution.py:292
  57.6 1.8 %collective-permute-start = (f32[2048,128]{1,0:T(8,128)}, f32[2048,128]{1,0:T(8,128)}, u32[]{:S(2)}, u32[]{:S(2)}) collective-permute-start(f32[2048,128]{1,0:T(8,128)} %get-tuple-element.25), channel_id=1, source_target_pairs={{0,2},{1,3},{2,0},{3,1},{4,6},{5,7},{6,4},{7,5}} | collective-permute-start | bytes 3145736 | tf_op jit(solution)/shard_map/ppermute | solution.py:478
  59.4 39.5 %weights.1 = (f32[8,2048,512]{2,1,0:T(8,128)}, f32[8,2048,512]{2,1,0:T(8,128)}, f32[8,512,2048]{2,1,0:T(8,128)}, f32[1,2048,512]{2,1,0:T(8,128)}, f32[1,2048,512]{2,1,0:T(8,128)}, /*index=5*/f32[1,512,2048]{2,1,0:T(8,128)}) custom-call(bf16[512,128]{1,0:T(8,128)(2,1)} %get-tuple-element.26.sdat, bf16[512,128]{1,0:T(8,128)(2,1)} %get-tuple-element.27.sdbt, ...), custom_call_target="tpu_custom_call" | custom-call | flops 12884901888 | bytes 130023424 | tf_op jit(solution)/shard_map/weights/pallas_call | solution.py:421
  98.9 0.0 collective-permute-done.back_h
  98.9 2.4 %final.1 = bf16[128,2048]{1,0:T(8,128)(2,1)} custom-call(f32[2048,128]{1,0:T(8,128)} %get-tuple-element.24.own_h, f32[2048,128]{1,0:T(8,128)} %collective-permute-done.back_h), custom_call_target="tpu_custom_call" | custom-call | tf_op jit(solution)/shard_map/final/pallas_call | solution.py:458
Async XLA Ops:
  57.6 41.3 %collective-permute-start = (f32[2048,128]{1,0:T(8,128)}, f32[2048,128]{1,0:T(8,128)}, u32[]{:S(2)}, u32[]{:S(2)}) collective-permute-start(f32[2048,128]{1,0:T(8,128)} %get-tuple-element.25), channel_id=1, source_target_pairs={{0,2},{1,3},{2,0},{3,1},{4,6},{5,7},{6,4},{7,5}} | collective-permute-start | bytes 3145736 | tf_op jit(solution)/shard_map/ppermute | solution.py:478

commit v5 on v4

--- a/solution.py
+++ b/solution.py
@@ -10,9 +10,9 @@
 MESH = pl.DeviceIdType.MESH
 SLOTS = 64
 COLS = 512
-RING, RING2 = 12, 8
+RING, RING2 = 16, 8
 OUTS = 5
-UP, DOWN, BACK = 4, 4, 4
+UP, DOWN, BACK = 4, 4, 8
 
 
 def dot(a, b):
@@ -27,14 +27,11 @@
     return pl.ds(pl.multiple_of(index * size, size), size)
 
 
-def swiglu_parts(a, b, g):
+def swiglu_factors(a, b):
     a, b = a.astype(F32), b.astype(F32)
     sigma = 0.5 * jnp.tanh(0.5 * a) + 0.5
     silu = a * sigma
-    hidden = (silu * b).astype(BF16)
-    grad_a = (g * b * (sigma + silu * (1.0 - sigma))).astype(BF16)
-    grad_b = (g * silu).astype(BF16)
-    return hidden, grad_a, grad_b
+    return (silu * b).astype(BF16), b * (sigma + silu * (1.0 - sigma)), silu
 
 
 def put_rows(got, q, rows):
@@ -127,8 +124,9 @@
         s_copy(k).wait()
     at = dot(x[...], s1v[...]).astype(BF16).astype(F32).T
     bt = dot(x[...], s3v[...]).astype(BF16).astype(F32).T
-    sht, sdat, sdbt = swiglu_parts(at, bt, dot_nt(s2v[...], dy[...]))
-    sht_o[...], sdat_o[...], sdbt_o[...] = sht, sdat, sdbt
+    grad = dot_nt(s2v[...], dy[...])
+    sht_o[...], by_a, by_b = swiglu_factors(at, bt)
+    sdat_o[...], sdbt_o[...] = (grad * by_a).astype(BF16), (grad * by_b).astype(BF16)
 
     def shared_back(m):
         own[span(m, COLS), :] = dot(s1v[span(m, COLS), :], sdat_o[...]) + dot(s3v[span(m, COLS), :], sdbt_o[...])
@@ -204,6 +202,14 @@
     each(chunks, up_chunk)
     near_copy(1).wait()
 
+    half = ff // 2
+
+    def prepare(e):
+        for h in range(2):
+            part = slice(h * half, (h + 1) * half)
+            a, b = acc[0, e, :, part].T.astype(BF16), acc[1, e, :, part].T.astype(BF16)
+            act[2, e, part, :], acc[0, e, :, part], acc[1, e, :, part] = swiglu_factors(a, b)
+
     def down_chunk(c):
         gather_chunk(1, c)
 
@@ -214,6 +220,7 @@
             parts = [dot_nt(w2ring[(base + k) % RING2], rows[DOWN * p + k]) for k in range(DOWN)]
             for k in range(DOWN):
                 gacc[DOWN * p + k] += parts[k]
+            prepare(c * (experts // DOWN) + p)
 
             @pl.when(base + RING2 < pieces)
             def _():
@@ -235,14 +242,13 @@
     for copy in outs:
         copy.start()
 
-    half = ff // 2
-
-    def middle(i):
-        e, part = i // 2, span(i % 2, half)
-        a, b = acc[0, e, :, part].T.astype(BF16), acc[1, e, :, part].T.astype(BF16)
-        act[2, e, part, :], act[0, e, part, :], act[1, e, part, :] = swiglu_parts(a, b, gacc[e, part, :])
-
-    each(2 * experts, middle)
+    def middle(e):
+        for h in range(2):
+            part = slice(h * half, (h + 1) * half)
+            for k in range(2):
+                act[k, e, part, :] = (gacc[e, part, :] * acc[k, e, :, part]).astype(BF16)
+
+    each(experts, middle)
     outs += [pltpu.make_async_copy(act.at[k], (dat_o, dbt_o, ht_o)[k], osem.at[6 + k]) for k in range(3)]
     for copy in outs[6:]:
         copy.start()

time: 101 us -> 96.7 us (0.957)
  Pallas kernels: 98.9 us -> 94.2 us
    pallas_call x1, Pallas kernels: 57 us -> 52.3 us  [exchange_call(): pl.pallas_call(exchange_kernel, in_specs=[vmem] * 5 + [hbm] * 6, out_spec...]
  transfers between devices with their start and end apart: 1 -> 1, of which waited for: 0 -> 0; matrix products, arithmetic and copies ran while one was open for 0% -> 0% of each run, Pallas kernels for 39% -> 41%
where the time goes in v5:
time: 96.7 us; the launch traced here: 96.5 us
  Pallas kernels  94.2 us (97%)
  starting transfers between devices  1.72 us (2%)
    pallas_call x1, Pallas kernels, exchange_call(): pl.pallas_call(exchange_kernel, in_specs=[vmem] * 5 + [hbm] * 6, out_spec...  52.3 us
    pallas_call x1, Pallas kernels, weight_call(): pl.pallas_call(weight_kernel, in_specs=[vmem] * 3 + [hbm] * 6, out_specs=...  39.5 us
    pallas_call x1, Pallas kernels, final_call(): pl.pallas_call(final_kernel, in_specs=[hbm, hbm], out_specs=hbm, out_shap...  2.37 us
  transfers between devices with their start and end apart: 1, of which 0 were waited for; matrix products, arithmetic and copies ran while one was open for 0% of the time, Pallas kernels for 41%

profile of v5, /device:TPU:0, one launch (start us, length us, event | category | flops | bytes accessed | tf_op | source)
XLA Modules:
  0.0 96.5 jit_solution(9422616002085712916)
XLA Ops:
  0.6 52.3 %exchange.1 = (bf16[8,512,256]{2,1,0:T(8,128)(2,1)}, bf16[8,512,256]{2,1,0:T(8,128)(2,1)}, bf16[8,512,256]{2,1,0:T(8,128)(2,1)}, bf16[2,4,128,2048]{3,2,1,0:T(8,...) custom-call(bf16[128,2048]{1,0:T(8,128)(2,1)} %x.1, ...), custom_call_target="tpu_custom_call" | custom-call | flops 25769803776 | bytes 100663296 | tf_op jit(solution)/shard_map/exchange/pallas_call | solution.py:298
  52.9 1.7 %collective-permute-start = (f32[2048,128]{1,0:T(8,128)}, f32[2048,128]{1,0:T(8,128)}, u32[]{:S(2)}, u32[]{:S(2)}) collective-permute-start(f32[2048,128]{1,0:T(8,128)} %get-tuple-element.25), channel_id=1, source_target_pairs={{0,2},{1,3},{2,0},{3,1},{4,6},{5,7},{6,4},{7,5}} | collective-permute-start | bytes 3145736 | tf_op jit(solution)/shard_map/ppermute | solution.py:484
  54.6 39.5 %weights.1 = (f32[8,2048,512]{2,1,0:T(8,128)}, f32[8,2048,512]{2,1,0:T(8,128)}, f32[8,512,2048]{2,1,0:T(8,128)}, f32[1,2048,512]{2,1,0:T(8,128)}, f32[1,2048,512]{2,1,0:T(8,128)}, /*index=5*/f32[1,512,2048]{2,1,0:T(8,128)}) custom-call(bf16[512,128]{1,0:T(8,128)(2,1)} %get-tuple-element.26.sdat, bf16[512,128]{1,0:T(8,128)(2,1)} %get-tuple-element.27.sdbt, ...), custom_call_target="tpu_custom_call" | custom-call | flops 12884901888 | bytes 130023424 | tf_op jit(solution)/shard_map/weights/pallas_call | solution.py:427
  94.2 0.0 collective-permute-done.back_h
  94.2 2.4 %final.1 = bf16[128,2048]{1,0:T(8,128)(2,1)} custom-call(f32[2048,128]{1,0:T(8,128)} %get-tuple-element.24.own_h, f32[2048,128]{1,0:T(8,128)} %collective-permute-done.back_h), custom_call_target="tpu_custom_call" | custom-call | tf_op jit(solution)/shard_map/final/pallas_call | solution.py:464
Async XLA Ops:
  52.9 41.2 %collective-permute-start = (f32[2048,128]{1,0:T(8,128)}, f32[2048,128]{1,0:T(8,128)}, u32[]{:S(2)}, u32[]{:S(2)}) collective-permute-start(f32[2048,128]{1,0:T(8,128)} %get-tuple-element.25), channel_id=1, source_target_pairs={{0,2},{1,3},{2,0},{3,1},{4,6},{5,7},{6,4},{7,5}} | collective-permute-start | bytes 3145736 | tf_op jit(solution)/shard_map/ppermute | solution.py:484

commit v6 on v5

--- a/solution.py
+++ b/solution.py
@@ -39,9 +39,9 @@
         rows[e, span(q, SLOTS), :] = got[e * SLOTS:(e + 1) * SLOTS]
 
 
-def exchange_kernel(x, dy, ids, slots, gates, w1, w3, w2, s1, s3, s2, dat_o, dbt_o, ht_o, tok_o, pick_o, gate_o, sdat_o, sdbt_o, sht_o, own, far,
-                    xg, yg, idg, slotg, gateg, wring, w2ring, s1v, s3v, s2v, acc, gacc, act, rows, pick, gate, ret, spread, sbuf, rbuf,
-                    near_s, near_r, far_s, far_r, hop_s, hop_r, tab_s, tab_r, sum_s, sum_r, wsem, w2sem, ssem, osem):
+def exchange_kernel(x, dy, ids, slots, gates, w1, w3, w2, s1, s3, s2, dat_o, dbt_o, ht_o, tok_o, pick_o, gate_o, own_o, far_o, sdat_o, sdbt_o, sht_o,
+                    xg, yg, idg, slotg, gateg, wring, w2ring, s1v, s3v, s2v, acc, gacc, act, rows, pick, gate, ret, spread, sbuf, rbuf, own, far,
+                    near_s, near_r, far_s, far_r, hop_s, hop_r, tab_s, tab_r, sum_s, sum_r, wsem, w2sem, ssem, osem, esem):
     me = lax.axis_index('ep')
     core = me % 2
     mate = me + 1 - 2 * core
@@ -83,8 +83,13 @@
 
     for k in range(3):
         s_copy(k).start()
-    each(RING, start_w)
-    each(RING2, lambda j: w2_copy(j).start())
+
+    def clear(e):
+        acc[0, e] = jnp.zeros_like(acc[0, e])
+        acc[1, e] = jnp.zeros_like(acc[1, e])
+        gacc[e] = jnp.zeros_like(gacc[e])
+
+    each(experts, clear)
 
     def remote(src, dst, send, recv, peer):
         return pltpu.make_async_remote_copy(src_ref=src, dst_ref=dst, send_sem=send, recv_sem=recv, device_id={'ep': peer}, device_id_type=MESH)
@@ -114,14 +119,9 @@
     near_copy(0).start()
     near_copy(1).start()
 
-    def clear(e):
-        acc[0, e] = jnp.zeros_like(acc[0, e])
-        acc[1, e] = jnp.zeros_like(acc[1, e])
-        gacc[e] = jnp.zeros_like(gacc[e])
-
-    each(experts, clear)
     for k in range(3):
         s_copy(k).wait()
+    each(RING // 2, start_w)
     at = dot(x[...], s1v[...]).astype(BF16).astype(F32).T
     bt = dot(x[...], s3v[...]).astype(BF16).astype(F32).T
     grad = dot_nt(s2v[...], dy[...])
@@ -131,6 +131,8 @@
     def shared_back(m):
         own[span(m, COLS), :] = dot(s1v[span(m, COLS), :], sdat_o[...]) + dot(s3v[span(m, COLS), :], sdbt_o[...])
 
+    each(RING // 2, lambda i: start_w(i + RING // 2))
+    each(RING2, lambda j: w2_copy(j).start())
     each(chunks, shared_back)
 
     for t in range(3):
@@ -277,14 +279,26 @@
         far[span(m, COLS), :] = keep[:, n:]
         sum_copy(m).start()
 
-    each(chunks, back_chunk)
+        @pl.when(m > 0)
+        def _():
+            add_mate(m - 1)
+
+    def out_copies(m):
+        at = span(m, COLS)
+        return pltpu.make_async_copy(own.at[at, :], own_o.at[at, :], esem.at[0, m]), pltpu.make_async_copy(far.at[at, :], far_o.at[at, :], esem.at[1, m])
 
     def add_mate(m):
         sum_copy(m).wait()
         own[span(m, COLS), :] += rbuf[m, :, :n]
         far[span(m, COLS), :] += rbuf[m, :, n:]
-
-    each(chunks, add_mate)
+        for copy in out_copies(m):
+            copy.start()
+
+    each(chunks, back_chunk)
+    add_mate(chunks - 1)
+    for m in range(chunks):
+        for copy in out_copies(m):
+            copy.wait()
     for copy in outs:
         copy.wait()
 
@@ -298,8 +312,8 @@
     return pl.pallas_call(
         exchange_kernel,
         in_specs=[vmem] * 5 + [hbm] * 6,
-        out_specs=[hbm] * 6 + [vmem] * 5,
-        out_shape=[jax.ShapeDtypeStruct((experts, ff, rows), BF16)] * 3 + [jax.ShapeDtypeStruct((2, 4, n, d), BF16), jax.ShapeDtypeStruct((4, experts * SLOTS, n), BF16), jax.ShapeDtypeStruct((4, experts * SLOTS, 1), F32)] + [jax.ShapeDtypeStruct((ff, n), BF16)] * 3 + [jax.ShapeDtypeStruct((d, n), F32)] * 2,
+        out_specs=[hbm] * 8 + [vmem] * 3,
+        out_shape=[jax.ShapeDtypeStruct((experts, ff, rows), BF16)] * 3 + [jax.ShapeDtypeStruct((2, 4, n, d), BF16), jax.ShapeDtypeStruct((4, experts * SLOTS, n), BF16), jax.ShapeDtypeStruct((4, experts * SLOTS, 1), F32)] + [jax.ShapeDtypeStruct((d, n), F32)] * 2 + [jax.ShapeDtypeStruct((ff, n), BF16)] * 3,
         scratch_shapes=[
             pltpu.VMEM((3, n, d), BF16), pltpu.VMEM((3, n, d), BF16), pltpu.VMEM((3,) + ids.shape, jnp.int32), pltpu.VMEM((3,) + ids.shape, jnp.int32), pltpu.VMEM((3,) + ids.shape, F32),
             pltpu.VMEM((RING, 2, COLS, ff), BF16), pltpu.VMEM((RING2, ff, COLS), BF16),
@@ -307,9 +321,9 @@
             pltpu.VMEM((2, experts, rows, ff), F32), pltpu.VMEM((experts, ff, rows), F32), pltpu.VMEM((3, experts, ff, rows), BF16),
             pltpu.VMEM((experts, rows, COLS), BF16), pltpu.VMEM((4, experts * SLOTS, n), BF16), pltpu.VMEM((4, experts * SLOTS, 1), F32),
             pltpu.VMEM((2, COLS, experts * 2 * SLOTS), BF16), pltpu.VMEM((2, experts * 2 * SLOTS, 2 * n), BF16),
-            pltpu.VMEM((chunks, COLS, 2 * n), F32), pltpu.VMEM((chunks, COLS, 2 * n), F32),
+            pltpu.VMEM((chunks, COLS, 2 * n), F32), pltpu.VMEM((chunks, COLS, 2 * n), F32), pltpu.VMEM((d, n), F32), pltpu.VMEM((d, n), F32),
             dma((2,)), dma((2,)), dma((2, chunks)), dma((2, chunks)), dma((2, chunks)), dma((2, chunks)), dma((3, 3)), dma((3, 3)), dma((chunks,)), dma((chunks,)),
-            dma((RING, 2)), dma((RING2,)), dma((3,)), dma((9,)),
+            dma((RING, 2)), dma((RING2,)), dma((3,)), dma((9,)), dma((2, chunks)),
         ],
         compiler_params=pltpu.CompilerParams(collective_id=0, has_side_effects=True, vmem_limit_bytes=67043328),
         cost_estimate=pl.CostEstimate(flops=12 * experts * rows * d * ff, bytes_accessed=96 * 2**20, transcendentals=0),
@@ -480,7 +494,7 @@
     group = mesh.shape['ep']
 
     def local_backward(x, dy, expert_ids, gate_vals, slot_pos, w1, w3, w2, s1, s3, s2):
-        dat, dbt, ht, tok, pick, gate, sdat, sdbt, sht, own, far = exchange_call(x, dy, expert_ids.T, slot_pos.T, gate_vals.T, w1, w3, w2, s1, s3, s2)
+        dat, dbt, ht, tok, pick, gate, own, far, sdat, sdbt, sht = exchange_call(x, dy, expert_ids.T, slot_pos.T, gate_vals.T, w1, w3, w2, s1, s3, s2)
         back = lax.ppermute(far, 'ep', [(i, i ^ 2) for i in range(group)])
         dw1, dw3, dw2, ds1, ds3, ds2 = weight_call(tok, pick, gate, dat, dbt, ht, sdat, sdbt, sht)
         grad_x = final_call(own, back)

time: 96.7 us -> 96.9 us (level)
  no operation moved by 1% of the time
where the time goes in v6:
time: 96.9 us; the launch traced here: 96.7 us
  Pallas kernels  94.8 us (98%)
  starting transfers between devices  1.22 us (1%)
    pallas_call x1, Pallas kernels, exchange_call(): pl.pallas_call(exchange_kernel, in_specs=[vmem] * 5 + [hbm] * 6, out_spec...  52.9 us
    pallas_call x1, Pallas kernels, weight_call(): pl.pallas_call(weight_kernel, in_specs=[vmem] * 3 + [hbm] * 6, out_specs=...  39.5 us
    pallas_call x1, Pallas kernels, final_call(): pl.pallas_call(final_kernel, in_specs=[hbm, hbm], out_specs=hbm, out_shap...  2.37 us
  transfers between devices with their start and end apart: 1, of which 0 were waited for; matrix products, arithmetic and copies ran while one was open for 0% of the time, Pallas kernels for 41%

profile of v6, /device:TPU:0, one launch (start us, length us, event | category | flops | bytes accessed | tf_op | source)
XLA Modules:
  0.0 96.7 jit_solution(15822517653088322028)
XLA Ops:
  0.6 52.9 %exchange.1 = (bf16[8,512,256]{2,1,0:T(8,128)(2,1)}, bf16[8,512,256]{2,1,0:T(8,128)(2,1)}, bf16[8,512,256]{2,1,0:T(8,128)(2,1)}, bf16[2,4,128,2048]{3,2,1,0:T(8,...) custom-call(bf16[128,2048]{1,0:T(8,128)(2,1)} %x.1, ...), custom_call_target="tpu_custom_call" | custom-call | flops 25769803776 | bytes 100663296 | tf_op jit(solution)/shard_map/exchange/pallas_call | solution.py:312
  53.6 1.2 %collective-permute-start = (f32[2048,128]{1,0:T(8,128)}, f32[2048,128]{1,0:T(8,128)}, u32[]{:S(2)}, u32[]{:S(2)}) collective-permute-start(f32[2048,128]{1,0:T(8,128)} %get-tuple-element.25), channel_id=1, source_target_pairs={{0,2},{1,3},{2,0},{3,1},{4,6},{5,7},{6,4},{7,5}} | collective-permute-start | bytes 3145736 | tf_op jit(solution)/shard_map/ppermute | solution.py:498
  54.8 39.5 %weights.1 = (f32[8,2048,512]{2,1,0:T(8,128)}, f32[8,2048,512]{2,1,0:T(8,128)}, f32[8,512,2048]{2,1,0:T(8,128)}, f32[1,2048,512]{2,1,0:T(8,128)}, f32[1,2048,512]{2,1,0:T(8,128)}, /*index=5*/f32[1,512,2048]{2,1,0:T(8,128)}) custom-call(bf16[512,128]{1,0:T(8,128)(2,1)} %get-tuple-element.26.sdat, bf16[512,128]{1,0:T(8,128)(2,1)} %get-tuple-element.27.sdbt, ...), custom_call_target="tpu_custom_call" | custom-call | flops 12884901888 | bytes 130023424 | tf_op jit(solution)/shard_map/weights/pallas_call | solution.py:441
  94.3 0.0 collective-permute-done.back_h
  94.3 2.4 %final.1 = bf16[128,2048]{1,0:T(8,128)(2,1)} custom-call(f32[2048,128]{1,0:T(8,128)} %get-tuple-element.24.own_h, f32[2048,128]{1,0:T(8,128)} %collective-permute-done.back_h), custom_call_target="tpu_custom_call" | custom-call | tf_op jit(solution)/shard_map/final/pallas_call | solution.py:478
Async XLA Ops:
  53.6 40.7 %collective-permute-start = (f32[2048,128]{1,0:T(8,128)}, f32[2048,128]{1,0:T(8,128)}, u32[]{:S(2)}, u32[]{:S(2)}) collective-permute-start(f32[2048,128]{1,0:T(8,128)} %get-tuple-element.25), channel_id=1, source_target_pairs={{0,2},{1,3},{2,0},{3,1},{4,6},{5,7},{6,4},{7,5}} | collective-permute-start | bytes 3145736 | tf_op jit(solution)/shard_map/ppermute | solution.py:498

commit v7 on v6

--- a/solution.py
+++ b/solution.py
@@ -10,7 +10,7 @@
 MESH = pl.DeviceIdType.MESH
 SLOTS = 64
 COLS = 512
-RING, RING2 = 16, 8
+RING, RING2 = 20, 12
 OUTS = 5
 UP, DOWN, BACK = 4, 4, 8
 
@@ -40,8 +40,8 @@
 
 
 def exchange_kernel(x, dy, ids, slots, gates, w1, w3, w2, s1, s3, s2, dat_o, dbt_o, ht_o, tok_o, pick_o, gate_o, own_o, far_o, sdat_o, sdbt_o, sht_o,
-                    xg, yg, idg, slotg, gateg, wring, w2ring, s1v, s3v, s2v, acc, gacc, act, rows, pick, gate, ret, spread, sbuf, rbuf, own, far,
-                    near_s, near_r, far_s, far_r, hop_s, hop_r, tab_s, tab_r, sum_s, sum_r, wsem, w2sem, ssem, osem, esem):
+                    xg, yg, idg, slotg, gateg, wring, w2ring, acc, gacc, act, rows, pick, gate, ret, spread, sbuf, rbuf, own, far,
+                    near_s, near_r, far_s, far_r, hop_s, hop_r, tab_s, tab_r, sum_s, sum_r, wsem, w2sem, osem, esem):
     me = lax.axis_index('ep')
     core = me % 2
     mate = me + 1 - 2 * core
@@ -63,8 +63,9 @@
     def w2_copy(j):
         return pltpu.make_async_copy(w2.at[j % experts, :, span(j // experts, COLS)], w2ring.at[j % RING2], w2sem.at[j % RING2])
 
-    def s_copy(k):
-        return pltpu.make_async_copy((s1, s3, s2)[k], (s1v, s3v, s2v)[k], ssem.at[k])
+    def s_copy(k, c):
+        src = s2.at[:, span(c, COLS)] if k == 2 else (s1, s3)[k].at[span(c, COLS), :]
+        return pltpu.make_async_copy(src, w2ring.at[k * chunks + c], w2sem.at[k * chunks + c])
 
     def each(count, body):
         def step(i, carry):
@@ -82,7 +83,7 @@
         w_copy(i, 1).wait()
 
     for k in range(3):
-        s_copy(k).start()
+        each(chunks, lambda c: s_copy(k, c).start())
 
     def clear(e):
         acc[0, e] = jnp.zeros_like(acc[0, e])
@@ -115,25 +116,38 @@
     for t in range(3):
         for k in range(3):
             tab_copy(t, k).start()
-    each(chunks, lambda c: far_copy(0, c).start())
+    far_copy(0, 0).start()
     near_copy(0).start()
     near_copy(1).start()
 
     for k in range(3):
-        s_copy(k).wait()
+        each(chunks, lambda c: s_copy(k, c).wait())
+    far_copy(0, 1).start()
     each(RING // 2, start_w)
-    at = dot(x[...], s1v[...]).astype(BF16).astype(F32).T
-    bt = dot(x[...], s3v[...]).astype(BF16).astype(F32).T
-    grad = dot_nt(s2v[...], dy[...])
+
+    def over_chunks(one):
+        total = one(0)
+        for c in range(1, chunks):
+            total += one(c)
+        return total
+
+    def cols(c):
+        return slice(c * COLS, (c + 1) * COLS)
+
+    at = over_chunks(lambda c: dot(x[:, cols(c)], w2ring[c])).astype(BF16).astype(F32).T
+    bt = over_chunks(lambda c: dot(x[:, cols(c)], w2ring[chunks + c])).astype(BF16).astype(F32).T
+    grad = over_chunks(lambda c: dot_nt(w2ring[2 * chunks + c], dy[:, cols(c)]))
     sht_o[...], by_a, by_b = swiglu_factors(at, bt)
     sdat_o[...], sdbt_o[...] = (grad * by_a).astype(BF16), (grad * by_b).astype(BF16)
+    far_copy(0, 2).start()
+    each(RING // 2, lambda i: start_w(i + RING // 2))
 
     def shared_back(m):
-        own[span(m, COLS), :] = dot(s1v[span(m, COLS), :], sdat_o[...]) + dot(s3v[span(m, COLS), :], sdbt_o[...])
-
-    each(RING // 2, lambda i: start_w(i + RING // 2))
+        own[span(m, COLS), :] = dot(w2ring[m], sdat_o[...]) + dot(w2ring[chunks + m], sdbt_o[...])
+
+    each(chunks, shared_back)
+    far_copy(0, 3).start()
     each(RING2, lambda j: w2_copy(j).start())
-    each(chunks, shared_back)
 
     for t in range(3):
         for k in range(3):
@@ -266,10 +280,11 @@
                 for h in range(2):
                     ret[h, :, span(e, 2 * SLOTS)] = part[:, h * 2 * SLOTS:(h + 1) * 2 * SLOTS]
 
-            @pl.when(base + RING < 2 * pieces)
-            def _():
-                for k in range(BACK):
-                    start_w(base + k + RING)
+            for half in (0, BACK // 2):
+                @pl.when(base + half + RING < 2 * pieces)
+                def _():
+                    for k in range(half, half + BACK // 2):
+                        start_w(base + k + RING)
 
         each(experts // BACK, back)
         give = dot(ret[1], spread[1])
@@ -317,13 +332,12 @@
         scratch_shapes=[
             pltpu.VMEM((3, n, d), BF16), pltpu.VMEM((3, n, d), BF16), pltpu.VMEM((3,) + ids.shape, jnp.int32), pltpu.VMEM((3,) + ids.shape, jnp.int32), pltpu.VMEM((3,) + ids.shape, F32),
             pltpu.VMEM((RING, 2, COLS, ff), BF16), pltpu.VMEM((RING2, ff, COLS), BF16),
-            pltpu.VMEM((d, ff), BF16), pltpu.VMEM((d, ff), BF16), pltpu.VMEM((ff, d), BF16),
             pltpu.VMEM((2, experts, rows, ff), F32), pltpu.VMEM((experts, ff, rows), F32), pltpu.VMEM((3, experts, ff, rows), BF16),
             pltpu.VMEM((experts, rows, COLS), BF16), pltpu.VMEM((4, experts * SLOTS, n), BF16), pltpu.VMEM((4, experts * SLOTS, 1), F32),
             pltpu.VMEM((2, COLS, experts * 2 * SLOTS), BF16), pltpu.VMEM((2, experts * 2 * SLOTS, 2 * n), BF16),
             pltpu.VMEM((chunks, COLS, 2 * n), F32), pltpu.VMEM((chunks, COLS, 2 * n), F32), pltpu.VMEM((d, n), F32), pltpu.VMEM((d, n), F32),
             dma((2,)), dma((2,)), dma((2, chunks)), dma((2, chunks)), dma((2, chunks)), dma((2, chunks)), dma((3, 3)), dma((3, 3)), dma((chunks,)), dma((chunks,)),
-            dma((RING, 2)), dma((RING2,)), dma((3,)), dma((9,)), dma((2, chunks)),
+            dma((RING, 2)), dma((RING2,)), dma((9,)), dma((2, chunks)),
         ],
         compiler_params=pltpu.CompilerParams(collective_id=0, has_side_effects=True, vmem_limit_bytes=67043328),
         cost_estimate=pl.CostEstimate(flops=12 * experts * rows * d * ff, bytes_accessed=96 * 2**20, transcendentals=0),

time: 96.9 us -> 97.4 us (level)
  no operation moved by 1% of the time
where the time goes in v7:
time: 97.4 us; the launch traced here: 97.2 us
  Pallas kernels  95.3 us (98%)
  starting transfers between devices  1.22 us (1%)
    pallas_call x1, Pallas kernels, exchange_call(): pl.pallas_call(exchange_kernel, in_specs=[vmem] * 5 + [hbm] * 6, out_spec...  53.4 us
    pallas_call x1, Pallas kernels, weight_call(): pl.pallas_call(weight_kernel, in_specs=[vmem] * 3 + [hbm] * 6, out_specs=...  39.5 us
    pallas_call x1, Pallas kernels, final_call(): pl.pallas_call(final_kernel, in_specs=[hbm, hbm], out_specs=hbm, out_shap...  2.37 us
  transfers between devices with their start and end apart: 1, of which 0 were waited for; matrix products, arithmetic and copies ran while one was open for 0% of the time, Pallas kernels for 41%

profile of v7, /device:TPU:0, one launch (start us, length us, event | category | flops | bytes accessed | tf_op | source)
XLA Modules:
  0.0 97.2 jit_solution(14759831064197344201)
XLA Ops:
  0.6 53.4 %exchange.1 = (bf16[8,512,256]{2,1,0:T(8,128)(2,1)}, bf16[8,512,256]{2,1,0:T(8,128)(2,1)}, bf16[8,512,256]{2,1,0:T(8,128)(2,1)}, bf16[2,4,128,2048]{3,2,1,0:T(8,...) custom-call(bf16[128,2048]{1,0:T(8,128)(2,1)} %x.1, ...), custom_call_target="tpu_custom_call" | custom-call | flops 25769803776 | bytes 100663296 | tf_op jit(solution)/shard_map/exchange/pallas_call | solution.py:327
  54.1 1.2 %collective-permute-start = (f32[2048,128]{1,0:T(8,128)}, f32[2048,128]{1,0:T(8,128)}, u32[]{:S(2)}, u32[]{:S(2)}) collective-permute-start(f32[2048,128]{1,0:T(8,128)} %get-tuple-element.25), channel_id=1, source_target_pairs={{0,2},{1,3},{2,0},{3,1},{4,6},{5,7},{6,4},{7,5}} | collective-permute-start | bytes 3145736 | tf_op jit(solution)/shard_map/ppermute | solution.py:512
  55.3 39.5 %weights.1 = (f32[8,2048,512]{2,1,0:T(8,128)}, f32[8,2048,512]{2,1,0:T(8,128)}, f32[8,512,2048]{2,1,0:T(8,128)}, f32[1,2048,512]{2,1,0:T(8,128)}, f32[1,2048,512]{2,1,0:T(8,128)}, /*index=5*/f32[1,512,2048]{2,1,0:T(8,128)}) custom-call(bf16[512,128]{1,0:T(8,128)(2,1)} %get-tuple-element.26.sdat, bf16[512,128]{1,0:T(8,128)(2,1)} %get-tuple-element.27.sdbt, ...), custom_call_target="tpu_custom_call" | custom-call | flops 12884901888 | bytes 130023424 | tf_op jit(solution)/shard_map/weights/pallas_call | solution.py:455
  94.8 0.0 collective-permute-done.back_h
  94.8 2.4 %final.1 = bf16[128,2048]{1,0:T(8,128)(2,1)} custom-call(f32[2048,128]{1,0:T(8,128)} %get-tuple-element.24.own_h, f32[2048,128]{1,0:T(8,128)} %collective-permute-done.back_h), custom_call_target="tpu_custom_call" | custom-call | tf_op jit(solution)/shard_map/final/pallas_call | solution.py:492
Async XLA Ops:
  54.1 40.7 %collective-permute-start = (f32[2048,128]{1,0:T(8,128)}, f32[2048,128]{1,0:T(8,128)}, u32[]{:S(2)}, u32[]{:S(2)}) collective-permute-start(f32[2048,128]{1,0:T(8,128)} %get-tuple-element.25), channel_id=1, source_target_pairs={{0,2},{1,3},{2,0},{3,1},{4,6},{5,7},{6,4},{7,5}} | collective-permute-start | bytes 3145736 | tf_op jit(solution)/shard_map/ppermute | solution.py:512

commit v8 on v7

--- a/solution.py
+++ b/solution.py
@@ -116,13 +116,12 @@
     for t in range(3):
         for k in range(3):
             tab_copy(t, k).start()
-    far_copy(0, 0).start()
+    each(chunks, lambda c: far_copy(0, c).start())
     near_copy(0).start()
     near_copy(1).start()
 
     for k in range(3):
         each(chunks, lambda c: s_copy(k, c).wait())
-    far_copy(0, 1).start()
     each(RING // 2, start_w)
 
     def over_chunks(one):
@@ -139,14 +138,12 @@
     grad = over_chunks(lambda c: dot_nt(w2ring[2 * chunks + c], dy[:, cols(c)]))
     sht_o[...], by_a, by_b = swiglu_factors(at, bt)
     sdat_o[...], sdbt_o[...] = (grad * by_a).astype(BF16), (grad * by_b).astype(BF16)
-    far_copy(0, 2).start()
     each(RING // 2, lambda i: start_w(i + RING // 2))
 
     def shared_back(m):
         own[span(m, COLS), :] = dot(w2ring[m], sdat_o[...]) + dot(w2ring[chunks + m], sdbt_o[...])
 
     each(chunks, shared_back)
-    far_copy(0, 3).start()
     each(RING2, lambda j: w2_copy(j).start())
 
     for t in range(3):
@@ -193,6 +190,14 @@
         gather_chunk(0, c)
 
         def up(p):
+            @pl.when((p == 1) & (c + 1 < chunks))
+            def _():
+                expect(0, c + 1)
+
+            @pl.when((p == 1) & (c + 1 == chunks))
+            def _():
+                expect(1, 0)
+
             base = c * experts + UP * p
             for k in range(UP):
                 wait_w(base + k)
@@ -203,17 +208,7 @@
             for k in range(UP):
                 start_w(base + k + RING)
 
-        each(experts // UP // 2, up)
-
-        @pl.when(c + 1 < chunks)
-        def _():
-            expect(0, c + 1)
-
-        @pl.when(c + 1 == chunks)
-        def _():
-            expect(1, 0)
-
-        each(experts // UP // 2, lambda p: up(p + experts // UP // 2))
+        each(experts // UP, up)
 
     each(chunks, up_chunk)
     near_copy(1).wait()
@@ -230,6 +225,10 @@
         gather_chunk(1, c)
 
         def down(p):
+            @pl.when((p == 1) & (c + 1 < chunks))
+            def _():
+                expect(1, c + 1)
+
             base = c * experts + DOWN * p
             for k in range(DOWN):
                 w2_copy(base + k).wait()
@@ -243,13 +242,7 @@
                 for k in range(DOWN):
                     w2_copy(base + k + RING2).start()
 
-        down(0)
-
-        @pl.when(c + 1 < chunks)
-        def _():
-            expect(1, c + 1)
-
-        each(experts // DOWN - 1, lambda p: down(p + 1))
+        each(experts // DOWN, down)
 
     each(chunks, down_chunk)
     outs = [pltpu.make_async_copy(x, tok_o.at[0, 0], osem.at[0]), pltpu.make_async_copy(xg, tok_o.at[0, 1:4], osem.at[1]),

time: 97.4 us -> 97.7 us (level)
  no operation moved by 1% of the time
where the time goes in v8:
time: 97.7 us; the launch traced here: 97.5 us
  Pallas kernels  95.6 us (98%)
  starting transfers between devices  1.22 us (1%)
    pallas_call x1, Pallas kernels, exchange_call(): pl.pallas_call(exchange_kernel, in_specs=[vmem] * 5 + [hbm] * 6, out_spec...  53.7 us
    pallas_call x1, Pallas kernels, weight_call(): pl.pallas_call(weight_kernel, in_specs=[vmem] * 3 + [hbm] * 6, out_specs=...  39.5 us
    pallas_call x1, Pallas kernels, final_call(): pl.pallas_call(final_kernel, in_specs=[hbm, hbm], out_specs=hbm, out_shap...  2.37 us
  transfers between devices with their start and end apart: 1, of which 0 were waited for; matrix products, arithmetic and copies ran while one was open for 0% of the time, Pallas kernels for 41%

profile of v8, /device:TPU:0, one launch (start us, length us, event | category | flops | bytes accessed | tf_op | source)
XLA Modules:
  0.0 97.5 jit_solution(12389566262092914269)
XLA Ops:
  0.6 53.7 %exchange.1 = (bf16[8,512,256]{2,1,0:T(8,128)(2,1)}, bf16[8,512,256]{2,1,0:T(8,128)(2,1)}, bf16[8,512,256]{2,1,0:T(8,128)(2,1)}, bf16[2,4,128,2048]{3,2,1,0:T(8,...) custom-call(bf16[128,2048]{1,0:T(8,128)(2,1)} %x.1, ...), custom_call_target="tpu_custom_call" | custom-call | flops 25769803776 | bytes 100663296 | tf_op jit(solution)/shard_map/exchange/pallas_call | solution.py:320
  54.4 1.2 %collective-permute-start = (f32[2048,128]{1,0:T(8,128)}, f32[2048,128]{1,0:T(8,128)}, u32[]{:S(2)}, u32[]{:S(2)}) collective-permute-start(f32[2048,128]{1,0:T(8,128)} %get-tuple-element.25), channel_id=1, source_target_pairs={{0,2},{1,3},{2,0},{3,1},{4,6},{5,7},{6,4},{7,5}} | collective-permute-start | bytes 3145736 | tf_op jit(solution)/shard_map/ppermute | solution.py:505
  55.6 39.5 %weights.1 = (f32[8,2048,512]{2,1,0:T(8,128)}, f32[8,2048,512]{2,1,0:T(8,128)}, f32[8,512,2048]{2,1,0:T(8,128)}, f32[1,2048,512]{2,1,0:T(8,128)}, f32[1,2048,512]{2,1,0:T(8,128)}, /*index=5*/f32[1,512,2048]{2,1,0:T(8,128)}) custom-call(bf16[512,128]{1,0:T(8,128)(2,1)} %get-tuple-element.26.sdat, bf16[512,128]{1,0:T(8,128)(2,1)} %get-tuple-element.27.sdbt, ...), custom_call_target="tpu_custom_call" | custom-call | flops 12884901888 | bytes 130023424 | tf_op jit(solution)/shard_map/weights/pallas_call | solution.py:448
  95.1 0.0 collective-permute-done.back_h
  95.1 2.4 %final.1 = bf16[128,2048]{1,0:T(8,128)(2,1)} custom-call(f32[2048,128]{1,0:T(8,128)} %get-tuple-element.24.own_h, f32[2048,128]{1,0:T(8,128)} %collective-permute-done.back_h), custom_call_target="tpu_custom_call" | custom-call | tf_op jit(solution)/shard_map/final/pallas_call | solution.py:485
Async XLA Ops:
  54.4 40.7 %collective-permute-start = (f32[2048,128]{1,0:T(8,128)}, f32[2048,128]{1,0:T(8,128)}, u32[]{:S(2)}, u32[]{:S(2)}) collective-permute-start(f32[2048,128]{1,0:T(8,128)} %get-tuple-element.25), channel_id=1, source_target_pairs={{0,2},{1,3},{2,0},{3,1},{4,6},{5,7},{6,4},{7,5}} | collective-permute-start | bytes 3145736 | tf_op jit(solution)/shard_map/ppermute | solution.py:505

commit v9 on v7

--- a/solution.py
+++ b/solution.py
@@ -10,9 +10,9 @@
 MESH = pl.DeviceIdType.MESH
 SLOTS = 64
 COLS = 512
-RING, RING2 = 20, 12
+RING, RING2 = 16, 16
 OUTS = 5
-UP, DOWN, BACK = 4, 4, 8
+BACK = 8
 
 
 def dot(a, b):
@@ -116,13 +116,12 @@
     for t in range(3):
         for k in range(3):
             tab_copy(t, k).start()
-    far_copy(0, 0).start()
+    each(chunks, lambda c: far_copy(0, c).start())
     near_copy(0).start()
     near_copy(1).start()
 
     for k in range(3):
         each(chunks, lambda c: s_copy(k, c).wait())
-    far_copy(0, 1).start()
     each(RING // 2, start_w)
 
     def over_chunks(one):
@@ -139,14 +138,12 @@
     grad = over_chunks(lambda c: dot_nt(w2ring[2 * chunks + c], dy[:, cols(c)]))
     sht_o[...], by_a, by_b = swiglu_factors(at, bt)
     sdat_o[...], sdbt_o[...] = (grad * by_a).astype(BF16), (grad * by_b).astype(BF16)
-    far_copy(0, 2).start()
     each(RING // 2, lambda i: start_w(i + RING // 2))
 
     def shared_back(m):
         own[span(m, COLS), :] = dot(w2ring[m], sdat_o[...]) + dot(w2ring[chunks + m], sdbt_o[...])
 
     each(chunks, shared_back)
-    far_copy(0, 3).start()
     each(RING2, lambda j: w2_copy(j).start())
 
     for t in range(3):
@@ -177,7 +174,6 @@
         hop_copy(a, c).start()
 
     def gather_chunk(a, c):
-        hop_copy(a, c).wait()
         for q in range(4):
             src = own_of[a] if q == 0 else got_of[a].at[q - 1]
             got = dot(pick[q], src[:, span(c, COLS)])
@@ -190,30 +186,26 @@
 
     def up_chunk(c):
         far_copy(1, c).start()
+        hop_copy(0, c).wait()
+
+        @pl.when(c + 1 < chunks)
+        def _():
+            expect(0, c + 1)
+
+        @pl.when(c + 1 == chunks)
+        def _():
+            expect(1, 0)
+
+        base = c * experts
+        for e in range(experts):
+            wait_w(base + e)
         gather_chunk(0, c)
-
-        def up(p):
-            base = c * experts + UP * p
-            for k in range(UP):
-                wait_w(base + k)
-            for k in range(UP):
-                e, i = UP * p + k, base + k
-                acc[0, e] += dot(rows[e], wring[i % RING, 0])
-                acc[1, e] += dot(rows[e], wring[i % RING, 1])
-            for k in range(UP):
-                start_w(base + k + RING)
-
-        each(experts // UP // 2, up)
-
-        @pl.when(c + 1 < chunks)
-        def _():
-            expect(0, c + 1)
-
-        @pl.when(c + 1 == chunks)
-        def _():
-            expect(1, 0)
-
-        each(experts // UP // 2, lambda p: up(p + experts // UP // 2))
+        for e in range(experts):
+            slot = (base + e) % RING
+            acc[0, e] += dot(rows[e], wring[slot, 0])
+            acc[1, e] += dot(rows[e], wring[slot, 1])
+        for e in range(experts):
+            start_w(base + e + RING)
 
     each(chunks, up_chunk)
     near_copy(1).wait()
@@ -227,29 +219,25 @@
             act[2, e, part, :], acc[0, e, :, part], acc[1, e, :, part] = swiglu_factors(a, b)
 
     def down_chunk(c):
+        hop_copy(1, c).wait()
+
+        @pl.when(c + 1 < chunks)
+        def _():
+            expect(1, c + 1)
+
+        base = c * experts
+        for e in range(experts):
+            w2_copy(base + e).wait()
         gather_chunk(1, c)
-
-        def down(p):
-            base = c * experts + DOWN * p
-            for k in range(DOWN):
-                w2_copy(base + k).wait()
-            parts = [dot_nt(w2ring[(base + k) % RING2], rows[DOWN * p + k]) for k in range(DOWN)]
-            for k in range(DOWN):
-                gacc[DOWN * p + k] += parts[k]
-            prepare(c * (experts // DOWN) + p)
-
-            @pl.when(base + RING2 < pieces)
-            def _():
-                for k in range(DOWN):
-                    w2_copy(base + k + RING2).start()
-
-        down(0)
-
-        @pl.when(c + 1 < chunks)
-        def _():
-            expect(1, c + 1)
-
-        each(experts // DOWN - 1, lambda p: down(p + 1))
+        for k in range(2):
+            prepare(2 * c + k)
+        for e in range(experts):
+            gacc[e] += dot_nt(w2ring[(base + e) % RING2], rows[e])
+
+        @pl.when(base + RING2 < pieces)
+        def _():
+            for e in range(experts):
+                w2_copy(base + e + RING2).start()
 
     each(chunks, down_chunk)
     outs = [pltpu.make_async_copy(x, tok_o.at[0, 0], osem.at[0]), pltpu.make_async_copy(xg, tok_o.at[0, 1:4], osem.at[1]),

time: 97.4 us -> 95.9 us (0.985)
  Pallas kernels: 95.3 us -> 93.9 us
    pallas_call x1, Pallas kernels: 53.4 us -> 52 us  [exchange_call(): pl.pallas_call(exchange_kernel, in_specs=[vmem] * 5 + [hbm] * 6, out_spec...]
where the time goes in v9:
time: 95.9 us; the launch traced here: 95.8 us
  Pallas kernels  93.9 us (98%)
  starting transfers between devices  1.22 us (1%)
    pallas_call x1, Pallas kernels, exchange_call(): pl.pallas_call(exchange_kernel, in_specs=[vmem] * 5 + [hbm] * 6, out_spec...  52 us
    pallas_call x1, Pallas kernels, weight_call(): pl.pallas_call(weight_kernel, in_specs=[vmem] * 3 + [hbm] * 6, out_specs=...  39.5 us
    pallas_call x1, Pallas kernels, final_call(): pl.pallas_call(final_kernel, in_specs=[hbm, hbm], out_specs=hbm, out_shap...  2.37 us
  transfers between devices with their start and end apart: 1, of which 0 were waited for; matrix products, arithmetic and copies ran while one was open for 0% of the time, Pallas kernels for 41%

profile of v9, /device:TPU:0, one launch (start us, length us, event | category | flops | bytes accessed | tf_op | source)
XLA Modules:
  0.0 95.8 jit_solution(898526579868542171)
XLA Ops:
  0.6 52.0 %exchange.1 = (bf16[8,512,256]{2,1,0:T(8,128)(2,1)}, bf16[8,512,256]{2,1,0:T(8,128)(2,1)}, bf16[8,512,256]{2,1,0:T(8,128)(2,1)}, bf16[2,4,128,2048]{3,2,1,0:T(8,...) custom-call(bf16[128,2048]{1,0:T(8,128)(2,1)} %x.1, ...), custom_call_target="tpu_custom_call" | custom-call | flops 25769803776 | bytes 100663296 | tf_op jit(solution)/shard_map/exchange/pallas_call | solution.py:315
  52.6 1.2 %collective-permute-start = (f32[2048,128]{1,0:T(8,128)}, f32[2048,128]{1,0:T(8,128)}, u32[]{:S(2)}, u32[]{:S(2)}) collective-permute-start(f32[2048,128]{1,0:T(8,128)} %get-tuple-element.25), channel_id=1, source_target_pairs={{0,2},{1,3},{2,0},{3,1},{4,6},{5,7},{6,4},{7,5}} | collective-permute-start | bytes 3145736 | tf_op jit(solution)/shard_map/ppermute | solution.py:500
  53.9 39.5 %weights.1 = (f32[8,2048,512]{2,1,0:T(8,128)}, f32[8,2048,512]{2,1,0:T(8,128)}, f32[8,512,2048]{2,1,0:T(8,128)}, f32[1,2048,512]{2,1,0:T(8,128)}, f32[1,2048,512]{2,1,0:T(8,128)}, /*index=5*/f32[1,512,2048]{2,1,0:T(8,128)}) custom-call(bf16[512,128]{1,0:T(8,128)(2,1)} %get-tuple-element.26.sdat, bf16[512,128]{1,0:T(8,128)(2,1)} %get-tuple-element.27.sdbt, ...), custom_call_target="tpu_custom_call" | custom-call | flops 12884901888 | bytes 130023424 | tf_op jit(solution)/shard_map/weights/pallas_call | solution.py:443
  93.4 0.0 collective-permute-done.back_h
  93.4 2.4 %final.1 = bf16[128,2048]{1,0:T(8,128)(2,1)} custom-call(f32[2048,128]{1,0:T(8,128)} %get-tuple-element.24.own_h, f32[2048,128]{1,0:T(8,128)} %collective-permute-done.back_h), custom_call_target="tpu_custom_call" | custom-call | tf_op jit(solution)/shard_map/final/pallas_call | solution.py:480
Async XLA Ops:
  52.6 40.7 %collective-permute-start = (f32[2048,128]{1,0:T(8,128)}, f32[2048,128]{1,0:T(8,128)}, u32[]{:S(2)}, u32[]{:S(2)}) collective-permute-start(f32[2048,128]{1,0:T(8,128)} %get-tuple-element.25), channel_id=1, source_target_pairs={{0,2},{1,3},{2,0},{3,1},{4,6},{5,7},{6,4},{7,5}} | collective-permute-start | bytes 3145736 | tf_op jit(solution)/shard_map/ppermute | solution.py:500

commit v10 on v9

--- a/solution.py
+++ b/solution.py
@@ -12,7 +12,6 @@
 COLS = 512
 RING, RING2 = 16, 16
 OUTS = 5
-BACK = 8
 
 
 def dot(a, b):
@@ -40,7 +39,7 @@
 
 
 def exchange_kernel(x, dy, ids, slots, gates, w1, w3, w2, s1, s3, s2, dat_o, dbt_o, ht_o, tok_o, pick_o, gate_o, own_o, far_o, sdat_o, sdbt_o, sht_o,
-                    xg, yg, idg, slotg, gateg, wring, w2ring, acc, gacc, act, rows, pick, gate, ret, spread, sbuf, rbuf, own, far,
+                    xg, yg, tabv, tabg, wring, w2ring, acc, gacc, act, rows, pick, gate, ret, spread, sbuf, rbuf, own, far,
                     near_s, near_r, far_s, far_r, hop_s, hop_r, tab_s, tab_r, sum_s, sum_r, wsem, w2sem, osem, esem):
     me = lax.axis_index('ep')
     core = me % 2
@@ -56,6 +55,12 @@
     for peer in (mate, other, diag):
         pl.semaphore_signal(barrier, inc=1, device_id={'ep': peer}, device_id_type=MESH)
 
+    tabv[...] = jnp.zeros_like(tabv)
+    top_k = ids.shape[0]
+    tabv[0, :top_k, :] = ids[...].astype(F32)
+    tabv[1, :top_k, :] = slots[...].astype(F32)
+    tabv[2, :top_k, :] = gates[...]
+
     def w_copy(i, k):
         src = (w1, w3)[k].at[i % experts, span((i // experts) % chunks, COLS), :]
         return pltpu.make_async_copy(src, wring.at[i % RING, k], wsem.at[i % RING, k])
@@ -106,16 +111,15 @@
     def hop_copy(a, c):
         return remote(got_of[a].at[0, :, span(c, COLS)], got_of[a].at[2, :, span(c, COLS)], hop_s.at[a, c], hop_r.at[a, c], mate)
 
-    def tab_copy(t, k):
-        return remote((ids, slots, gates)[t], (idg, slotg, gateg)[t].at[k], tab_s.at[t, k], tab_r.at[t, k], (other, mate, diag)[k])
+    def tab_copy(k):
+        return remote(tabv, tabg.at[k], tab_s.at[k], tab_r.at[k], (other, mate, diag)[k])
 
     def sum_copy(m):
         return remote(sbuf.at[m], rbuf.at[m], sum_s.at[m], sum_r.at[m], mate)
 
     pl.semaphore_wait(barrier, 3)
-    for t in range(3):
-        for k in range(3):
-            tab_copy(t, k).start()
+    for k in range(3):
+        tab_copy(k).start()
     each(chunks, lambda c: far_copy(0, c).start())
     near_copy(0).start()
     near_copy(1).start()
@@ -146,19 +150,18 @@
     each(chunks, shared_back)
     each(RING2, lambda j: w2_copy(j).start())
 
-    for t in range(3):
-        for k in range(3):
-            tab_copy(t, k).wait()
-    mine = me * experts + lax.broadcasted_iota(jnp.int32, (experts, n), 0)
-    rank = lax.broadcasted_iota(jnp.int32, (SLOTS, n), 0)
+    for k in range(3):
+        tab_copy(k).wait()
+    mine = (me * experts + lax.broadcasted_iota(jnp.int32, (experts, n), 0)).astype(F32)
+    rank = lax.broadcasted_iota(jnp.int32, (SLOTS, n), 0).astype(F32)
     for q in range(4):
-        idq, slotq, gateq = (ids, slots, gates) if q == 0 else (idg.at[q - 1], slotg.at[q - 1], gateg.at[q - 1])
-        slot = jnp.full((experts, n), -1, jnp.int32)
+        tabq = tabv if q == 0 else tabg.at[q - 1]
+        slot = jnp.full((experts, n), -1.0, F32)
         weight = jnp.zeros((experts, n), F32)
         for j in range(ids.shape[0]):
-            hit = mine == idq[j:j + 1, :]
-            slot = jnp.where(hit, slotq[j:j + 1, :], slot)
-            weight = jnp.where(hit, gateq[j:j + 1, :], weight)
+            hit = mine == tabq[0, j:j + 1, :]
+            slot = jnp.where(hit, tabq[1, j:j + 1, :], slot)
+            weight = jnp.where(hit, tabq[2, j:j + 1, :], weight)
         for e in range(experts):
             hit = rank == slot[e:e + 1, :]
             pick[q, e * SLOTS:(e + 1) * SLOTS, :] = jnp.where(hit, 1.0, 0.0).astype(BF16)
@@ -258,29 +261,26 @@
         copy.start()
 
     def back_chunk(m):
-        def back(p):
-            base = pieces + m * experts + BACK * p
-            for k in range(BACK):
-                wait_w(base + k)
-            for k in range(BACK):
-                e, i = BACK * p + k, base + k
-                part = (dot(wring[i % RING, 0], act[0, e]) + dot(wring[i % RING, 1], act[1, e])).astype(BF16)
-                for h in range(2):
-                    ret[h, :, span(e, 2 * SLOTS)] = part[:, h * 2 * SLOTS:(h + 1) * 2 * SLOTS]
-
-            for half in (0, BACK // 2):
-                @pl.when(base + half + RING < 2 * pieces)
-                def _():
-                    for k in range(half, half + BACK // 2):
-                        start_w(base + k + RING)
-
-        each(experts // BACK, back)
+        base = pieces + m * experts
+        for e in range(experts):
+            wait_w(base + e)
+        for e in range(experts):
+            slot = (base + e) % RING
+            part = (dot(wring[slot, 0], act[0, e]) + dot(wring[slot, 1], act[1, e])).astype(BF16)
+            for h in range(2):
+                ret[h, :, e * 2 * SLOTS:(e + 1) * 2 * SLOTS] = part[:, h * 2 * SLOTS:(h + 1) * 2 * SLOTS]
         give = dot(ret[1], spread[1])
         keep = dot(ret[0], spread[0])
         sbuf[m] = give
         own[span(m, COLS), :] += keep[:, :n]
         far[span(m, COLS), :] = keep[:, n:]
         sum_copy(m).start()
+
+        for half in (0, experts // 2):
+            @pl.when(base + half + RING < 2 * pieces)
+            def _():
+                for k in range(half, half + experts // 2):
+                    start_w(base + k + RING)
 
         @pl.when(m > 0)
         def _():
@@ -318,13 +318,13 @@
         out_specs=[hbm] * 8 + [vmem] * 3,
         out_shape=[jax.ShapeDtypeStruct((experts, ff, rows), BF16)] * 3 + [jax.ShapeDtypeStruct((2, 4, n, d), BF16), jax.ShapeDtypeStruct((4, experts * SLOTS, n), BF16), jax.ShapeDtypeStruct((4, experts * SLOTS, 1), F32)] + [jax.ShapeDtypeStruct((d, n), F32)] * 2 + [jax.ShapeDtypeStruct((ff, n), BF16)] * 3,
         scratch_shapes=[
-            pltpu.VMEM((3, n, d), BF16), pltpu.VMEM((3, n, d), BF16), pltpu.VMEM((3,) + ids.shape, jnp.int32), pltpu.VMEM((3,) + ids.shape, jnp.int32), pltpu.VMEM((3,) + ids.shape, F32),
+            pltpu.VMEM((3, n, d), BF16), pltpu.VMEM((3, n, d), BF16), pltpu.VMEM((3, 16, n), F32), pltpu.VMEM((3, 3, 16, n), F32),
             pltpu.VMEM((RING, 2, COLS, ff), BF16), pltpu.VMEM((RING2, ff, COLS), BF16),
             pltpu.VMEM((2, experts, rows, ff), F32), pltpu.VMEM((experts, ff, rows), F32), pltpu.VMEM((3, experts, ff, rows), BF16),
             pltpu.VMEM((experts, rows, COLS), BF16), pltpu.VMEM((4, experts * SLOTS, n), BF16), pltpu.VMEM((4, experts * SLOTS, 1), F32),
             pltpu.VMEM((2, COLS, experts * 2 * SLOTS), BF16), pltpu.VMEM((2, experts * 2 * SLOTS, 2 * n), BF16),
             pltpu.VMEM((chunks, COLS, 2 * n), F32), pltpu.VMEM((chunks, COLS, 2 * n), F32), pltpu.VMEM((d, n), F32), pltpu.VMEM((d, n), F32),
-            dma((2,)), dma((2,)), dma((2, chunks)), dma((2, chunks)), dma((2, chunks)), dma((2, chunks)), dma((3, 3)), dma((3, 3)), dma((chunks,)), dma((chunks,)),
+            dma((2,)), dma((2,)), dma((2, chunks)), dma((2, chunks)), dma((2, chunks)), dma((2, chunks)), dma((3,)), dma((3,)), dma((chunks,)), dma((chunks,)),
             dma((RING, 2)), dma((RING2,)), dma((9,)), dma((2, chunks)),
         ],
         compiler_params=pltpu.CompilerParams(collective_id=0, has_side_effects=True, vmem_limit_bytes=67043328),

time: 95.9 us -> 95.7 us (level)
  no operation moved by 1% of the time
where the time goes in v10:
time: 95.7 us; the launch traced here: 95.6 us
  Pallas kernels  93.7 us (98%)
  starting transfers between devices  1.16 us (1%)
    pallas_call x1, Pallas kernels, exchange_call(): pl.pallas_call(exchange_kernel, in_specs=[vmem] * 5 + [hbm] * 6, out_spec...  51.9 us
    pallas_call x1, Pallas kernels, weight_call(): pl.pallas_call(weight_kernel, in_specs=[vmem] * 3 + [hbm] * 6, out_specs=...  39.5 us
    pallas_call x1, Pallas kernels, final_call(): pl.pallas_call(final_kernel, in_specs=[hbm, hbm], out_specs=hbm, out_shap...  2.37 us
  transfers between devices with their start and end apart: 1, of which 0 were waited for; matrix products, arithmetic and copies ran while one was open for 0% of the time, Pallas kernels for 41%

profile of v10, /device:TPU:0, one launch (start us, length us, event | category | flops | bytes accessed | tf_op | source)
XLA Modules:
  0.0 95.6 jit_solution(7827729442872706843)
XLA Ops:
  0.6 51.9 %exchange.1 = (bf16[8,512,256]{2,1,0:T(8,128)(2,1)}, bf16[8,512,256]{2,1,0:T(8,128)(2,1)}, bf16[8,512,256]{2,1,0:T(8,128)(2,1)}, bf16[2,4,128,2048]{3,2,1,0:T(8,...) custom-call(bf16[128,2048]{1,0:T(8,128)(2,1)} %x.1, ...), custom_call_target="tpu_custom_call" | custom-call | flops 25769803776 | bytes 100663296 | tf_op jit(solution)/shard_map/exchange/pallas_call | solution.py:315
  52.5 1.2 %collective-permute-start = (f32[2048,128]{1,0:T(8,128)}, f32[2048,128]{1,0:T(8,128)}, u32[]{:S(2)}, u32[]{:S(2)}) collective-permute-start(f32[2048,128]{1,0:T(8,128)} %get-tuple-element.25), channel_id=1, source_target_pairs={{0,2},{1,3},{2,0},{3,1},{4,6},{5,7},{6,4},{7,5}} | collective-permute-start | bytes 3145736 | tf_op jit(solution)/shard_map/ppermute | solution.py:500
  53.7 39.5 %weights.1 = (f32[8,2048,512]{2,1,0:T(8,128)}, f32[8,2048,512]{2,1,0:T(8,128)}, f32[8,512,2048]{2,1,0:T(8,128)}, f32[1,2048,512]{2,1,0:T(8,128)}, f32[1,2048,512]{2,1,0:T(8,128)}, /*index=5*/f32[1,512,2048]{2,1,0:T(8,128)}) custom-call(bf16[512,128]{1,0:T(8,128)(2,1)} %get-tuple-element.26.sdat, bf16[512,128]{1,0:T(8,128)(2,1)} %get-tuple-element.27.sdbt, ...), custom_call_target="tpu_custom_call" | custom-call | flops 12884901888 | bytes 130023424 | tf_op jit(solution)/shard_map/weights/pallas_call | solution.py:443
  93.2 0.0 collective-permute-done.back_h
  93.2 2.4 %final.1 = bf16[128,2048]{1,0:T(8,128)(2,1)} custom-call(f32[2048,128]{1,0:T(8,128)} %get-tuple-element.24.own_h, f32[2048,128]{1,0:T(8,128)} %collective-permute-done.back_h), custom_call_target="tpu_custom_call" | custom-call | tf_op jit(solution)/shard_map/final/pallas_call | solution.py:480
Async XLA Ops:
  52.5 40.7 %collective-permute-start = (f32[2048,128]{1,0:T(8,128)}, f32[2048,128]{1,0:T(8,128)}, u32[]{:S(2)}, u32[]{:S(2)}) collective-permute-start(f32[2048,128]{1,0:T(8,128)} %get-tuple-element.25), channel_id=1, source_target_pairs={{0,2},{1,3},{2,0},{3,1},{4,6},{5,7},{6,4},{7,5}} | collective-permute-start | bytes 3145736 | tf_op jit(solution)/shard_map/ppermute | solution.py:500

commit v11 on v10

--- a/solution.py
+++ b/solution.py
@@ -191,7 +191,7 @@
         far_copy(1, c).start()
         hop_copy(0, c).wait()
 
-        @pl.when(c + 1 < chunks)
+        @pl.when((c > 0) & (c + 1 < chunks))
         def _():
             expect(0, c + 1)
 
@@ -209,6 +209,10 @@
             acc[1, e] += dot(rows[e], wring[slot, 1])
         for e in range(experts):
             start_w(base + e + RING)
+
+        @pl.when(c == 0)
+        def _():
+            expect(0, 1)
 
     each(chunks, up_chunk)
     near_copy(1).wait()

time: 95.7 us -> 95.6 us (level)
  no operation moved by 1% of the time
where the time goes in v11:
time: 95.6 us; the launch traced here: 95.4 us
  Pallas kernels  93.6 us (98%)
  starting transfers between devices  1.16 us (1%)
    pallas_call x1, Pallas kernels, exchange_call(): pl.pallas_call(exchange_kernel, in_specs=[vmem] * 5 + [hbm] * 6, out_spec...  51.7 us
    pallas_call x1, Pallas kernels, weight_call(): pl.pallas_call(weight_kernel, in_specs=[vmem] * 3 + [hbm] * 6, out_specs=...  39.5 us
    pallas_call x1, Pallas kernels, final_call(): pl.pallas_call(final_kernel, in_specs=[hbm, hbm], out_specs=hbm, out_shap...  2.37 us
  transfers between devices with their start and end apart: 1, of which 0 were waited for; matrix products, arithmetic and copies ran while one was open for 0% of the time, Pallas kernels for 41%

profile of v11, /device:TPU:0, one launch (start us, length us, event | category | flops | bytes accessed | tf_op | source)
XLA Modules:
  0.0 95.4 jit_solution(6570974771564655522)
XLA Ops:
  0.6 51.7 %exchange.1 = (bf16[8,512,256]{2,1,0:T(8,128)(2,1)}, bf16[8,512,256]{2,1,0:T(8,128)(2,1)}, bf16[8,512,256]{2,1,0:T(8,128)(2,1)}, bf16[2,4,128,2048]{3,2,1,0:T(8,...) custom-call(bf16[128,2048]{1,0:T(8,128)(2,1)} %x.1, ...), custom_call_target="tpu_custom_call" | custom-call | flops 25769803776 | bytes 100663296 | tf_op jit(solution)/shard_map/exchange/pallas_call | solution.py:319
  52.3 1.2 %collective-permute-start = (f32[2048,128]{1,0:T(8,128)}, f32[2048,128]{1,0:T(8,128)}, u32[]{:S(2)}, u32[]{:S(2)}) collective-permute-start(f32[2048,128]{1,0:T(8,128)} %get-tuple-element.25), channel_id=1, source_target_pairs={{0,2},{1,3},{2,0},{3,1},{4,6},{5,7},{6,4},{7,5}} | collective-permute-start | bytes 3145736 | tf_op jit(solution)/shard_map/ppermute | solution.py:504
  53.5 39.5 %weights.1 = (f32[8,2048,512]{2,1,0:T(8,128)}, f32[8,2048,512]{2,1,0:T(8,128)}, f32[8,512,2048]{2,1,0:T(8,128)}, f32[1,2048,512]{2,1,0:T(8,128)}, f32[1,2048,512]{2,1,0:T(8,128)}, /*index=5*/f32[1,512,2048]{2,1,0:T(8,128)}) custom-call(bf16[512,128]{1,0:T(8,128)(2,1)} %get-tuple-element.26.sdat, bf16[512,128]{1,0:T(8,128)(2,1)} %get-tuple-element.27.sdbt, ...), custom_call_target="tpu_custom_call" | custom-call | flops 12884901888 | bytes 130023424 | tf_op jit(solution)/shard_map/weights/pallas_call | solution.py:447
  93.0 0.0 collective-permute-done.back_h
  93.0 2.4 %final.1 = bf16[128,2048]{1,0:T(8,128)(2,1)} custom-call(f32[2048,128]{1,0:T(8,128)} %get-tuple-element.24.own_h, f32[2048,128]{1,0:T(8,128)} %collective-permute-done.back_h), custom_call_target="tpu_custom_call" | custom-call | tf_op jit(solution)/shard_map/final/pallas_call | solution.py:484
Async XLA Ops:
  52.3 40.7 %collective-permute-start = (f32[2048,128]{1,0:T(8,128)}, f32[2048,128]{1,0:T(8,128)}, u32[]{:S(2)}, u32[]{:S(2)}) collective-permute-start(f32[2048,128]{1,0:T(8,128)} %get-tuple-element.25), channel_id=1, source_target_pairs={{0,2},{1,3},{2,0},{3,1},{4,6},{5,7},{6,4},{7,5}} | collective-permute-start | bytes 3145736 | tf_op jit(solution)/shard_map/ppermute | solution.py:504
